TPU v7x, 32 devices: a whole 2x2x4 slice. The times are simulated.
32 devices in a mesh: solver: 4 (over y, x), space: 8 (over z, core).
Axes of the slice: x: 2, y: 2, z: 4, core: 2. Of those that a mesh axis runs over, the one named last changes fastest.
Arguments:
- pressure_start: float32 [128, 256, 512], P(('solver', 'space')), may hold values from -6 to 6
- fluid_coef: float32 [128, 256, 512], P(('solver', 'space')), may hold values from 0.25 to 2
- fluid_rhs: float32 [128, 256, 512], P(('solver', 'space')), may hold values from -6 to 6
- wall_start: float32 [3, 8, 128, 256], P(None, None, ('solver', 'space')), may hold values from -4 to 4
- wall_stiff: float32 [8, 128, 256], P(None, ('solver', 'space')), may hold values from 0.5 to 4
- wall_load: float32 [3, 8, 128, 256], P(None, None, ('solver', 'space')), may hold values from -6 to 6
- normals: float32 [3, 32768], P(None, ('solver', 'space')), may hold values from -4 to 4
- fluid_owner: int32 [32768, 1], P(('solver', 'space')), may hold values from 0 to 31; in each aligned block of 1024 rows (0 to 1023, 1024 to 2047, ...) at most 64 rows name the same one
- fluid_cell: int32 [32768], P(('solver', 'space')), may hold values from 0 to 524287
- interface_start: float32 [6, 32768], P(None, ('solver', 'space')), may hold values from -6 to 6
- past_residual: float32 [32, 6, 32768], P(None, None, ('solver', 'space')), may hold values from -4 to 4
- past_output: float32 [32, 6, 32768], P(None, None, ('solver', 'space')), may hold values from -4 to 4
Outputs:
- interface_next: float32 [6, 32768], P(None, ('solver', 'space'))
- pressure: float32 [128, 256, 512], P(('solver', 'space'))
- wall: float32 [3, 8, 128, 256], P(None, None, ('solver', 'space'))
Inputs may be any that keep to these rules, and one draw needn't show every extreme that they name: `fluid_owner`: among the 1024 interface points of one device, at most 64 have the same fluid owner.
All inputs are finite; a program needn't handle non-finite values.
Results may differ from a plain program's by a relative error of at most 0.00011.
Values sent between devices are 32-bit elements; how exact they have to be, the bound alone decides.
No kernel may reach another device: no remote copies, remote signals or barrier semaphores. Data moves between devices by JAX's collectives and lax.ppermute only.
A program may use at most 64 MiB of HBM per device.

v0:
```python
import functools

import jax
import jax.numpy as jnp
from jax import lax
from jax.experimental import pallas as pl
from jax.experimental.pallas import tpu as pltpu
from jax.sharding import PartitionSpec as P


SWEEPS = 4
COUPLE = 2

OMEGA = 0.8
SOURCE_GAIN = 4.0
RIDGE = 0.1
TINY = 1e-06

AXES = ("solver", "space")
LANES = 128
GRIDS = 4
SUB = 8
HIGHEST = lax.Precision.HIGHEST
F32 = jnp.float32


def vmem():
    return pl.BlockSpec(memory_space=pltpu.VMEM)


def smem():
    return pl.BlockSpec(memory_space=pltpu.SMEM)


def call(kernel, outs, ins, scratch=(), limit=16):
    return pl.pallas_call(
        kernel,
        out_shape=[jax.ShapeDtypeStruct(shape, dtype) for shape, dtype in outs],
        in_specs=ins,
        out_specs=[vmem() for _ in outs],
        scratch_shapes=list(scratch),
        compiler_params=pltpu.CompilerParams(vmem_limit_bytes=limit * 1024 * 1024),
    )


def dot(a, b, dims):
    return lax.dot_general(a, b, (dims, ((), ())), precision=HIGHEST, preferred_element_type=F32)


def iota(shape, dim):
    return lax.broadcasted_iota(jnp.int32, shape, dim)


def exchange(send):
    return lax.all_to_all(send, AXES, split_axis=0, concat_axis=0, tiled=True)


def tie(*values):
    return lax.optimization_barrier(values)


def pairs():
    count = lax.axis_size(AXES)
    near = [(i, i ^ 1) for i in range(count)]
    up = [(i, i + 1) for i in range(1, count - 1, 2)]
    return near, up + [(target, source) for source, target in up]


def swap(near, far):
    first, second = pairs()
    return lax.ppermute(near, AXES, first), lax.ppermute(far, AXES, second)


def onehots(owner, rank, devices, most):
    points = owner.shape[1]
    named = (owner == iota((devices, points), 0)).astype(F32)
    placed = (rank == iota((most, points), 0)).astype(F32)
    return named, placed


def flux_of(normals, state):
    product = normals * state[0:3]
    return SOURCE_GAIN * (product[0:1] + product[1:2] + product[2:3])


def route_kernel(devices, most, owner_ref, cell_ref, normals_ref, state_ref, send_ref, rank_ref):
    points = owner_ref.shape[1]
    owner = owner_ref[...]
    named = (owner == iota((devices, points), 0)).astype(F32)
    blocks = [named[:, i * LANES : (i + 1) * LANES] for i in range(points // LANES)]
    earlier = (iota((LANES, LANES), 0) < iota((LANES, LANES), 1)).astype(jnp.bfloat16)
    base = jnp.zeros((devices, 1), F32)
    for i, block in enumerate(blocks):
        ahead = jnp.dot(block.astype(jnp.bfloat16), earlier, preferred_element_type=F32) + base
        rank_ref[:, i * LANES : (i + 1) * LANES] = jnp.sum(ahead * block, axis=0, keepdims=True).astype(jnp.int32)
        base = base + jnp.sum(block, axis=1, keepdims=True)
    placed = (rank_ref[...] == iota((most, points), 0)).astype(F32)
    flux = flux_of(normals_ref[...], state_ref[...])
    marks = (cell_ref[...] + 1).astype(F32)
    send_ref[...] = jnp.zeros_like(send_ref)
    send_ref[:, 0:most] = dot(named, placed * marks, ((1,), (1,)))
    send_ref[:, most : 2 * most] = dot(named, placed * flux, ((1,), (1,)))


def tiled_place(cell, depth):
    across = depth // LANES
    row, along = cell // depth, cell % depth
    tile = (row // SUB) * across + along // LANES
    return (tile * SUB + row % SUB) * LANES + along % LANES


def scatter_cells(most, first, code_ref, value_ref, grids):
    count = len(grids)
    place = iota((SUB, LANES), 0) * LANES + iota((SUB, LANES), 1)
    area = SUB * LANES
    fill = 8

    def clear(step, carry):
        for grid in grids:
            grid[pl.ds(step * fill, fill)] = jnp.zeros((fill, SUB, LANES), F32)
        return carry

    lax.fori_loop(0, grids[0].shape[0] // fill, clear, 0)
    part = code_ref.shape[0] // count

    def outer(d, carry):
        for slot in range(most):
            codes = [code_ref[g * part + d, slot] for g in range(count)]
            tiles = [lax.shift_right_logical(code, area.bit_length() - 1) for code in codes]
            added = [
                grid[tile] + jnp.where(place == (code & (area - 1)), value_ref[g * part + d, first + slot], 0.0)
                for g, (grid, tile, code) in enumerate(zip(grids, tiles, codes))
            ]
            for grid, tile, new in zip(grids, tiles, added):
                grid[tile] = new
        return carry

    lax.fori_loop(0, part, outer, 0)


def gather_cells(most, code_ref, flat_ref, extra_ref, out_ref, lines_ref):
    devices = code_ref.shape[0]
    lane = iota((1, LANES), 1)
    unroll = 16

    def outer(d, carry):
        base = pl.multiple_of(d * most, SUB)
        for low in range(0, most, unroll):
            found = []
            for k in range(min(unroll, most - low)):
                code = code_ref[d, low + k]
                line = flat_ref[pl.ds(lax.shift_right_logical(code, LANES.bit_length() - 1), 1), :]
                found.append(jnp.where(lane == (code & (LANES - 1)), line, 0.0))
            for k, line in enumerate(found):
                lines_ref[pl.ds(base + (low + k), 1), :] = line
        return carry

    lax.fori_loop(0, devices, outer, 0)
    ones = jnp.ones((SUB, LANES), F32)
    found = dot(ones, lines_ref[...], ((1,), (1,)))
    out_ref[...] = jnp.zeros_like(out_ref)
    if extra_ref is not None:
        out_ref[:, most : most + 2] = jnp.broadcast_to(extra_ref[0:1, 0:2], (devices, 2))
    for d in range(devices):
        out_ref[d : d + 1, 0:most] = found[0:1, d * most : (d + 1) * most]


def gather_kernel(most, code_ref, field_ref, out_ref, lines_ref, flat_ref):
    across = field_ref.shape[1] // LANES

    def flatten(j, carry):
        for k in range(2):
            for t in range(across):
                to = pl.ds(pl.multiple_of(((2 * j + k) * across + t) * SUB, SUB), SUB)
                at = pl.ds(pl.multiple_of((2 * j + k) * SUB, SUB), SUB)
                flat_ref[to, :] = field_ref[at, t * LANES : (t + 1) * LANES]
        return carry

    lax.fori_loop(0, field_ref.shape[0] // (2 * SUB), flatten, 0)
    gather_cells(most, code_ref, flat_ref, None, out_ref, lines_ref)


def sweep_kernel(rows, most, first, opening, closing, sending, carrying, *refs):
    refs = list(refs)
    me_ref, field_ref, near_ref, far_ref, rhs_ref, scale_ref = refs[:6]
    del refs[:6]
    if opening or closing:
        code_ref = refs.pop(0)
    if opening:
        value_ref = refs.pop(0)
    extra_ref = refs.pop(0) if closing and carrying else None
    out_ref = refs.pop(0)
    sends = [refs.pop(0), refs.pop(0)] if sending else []
    grids = []
    if opening:
        source_ref, *grids = refs
        scatter_cells(most, first, code_ref, value_ref, grids)
    if closing:
        sampled_ref, lines_ref, flat_ref = refs
    wide, depth = near_ref.shape
    across = depth // LANES
    sub = iota((SUB, depth), 0)
    lane = iota((SUB, depth), 1)
    even = (me_ref[0] & 1) == 0
    blocks = wide // SUB
    unroll = 2

    def block(j):
        y = pl.multiple_of(j * SUB, SUB)
        above = pl.multiple_of(jnp.maximum(j - 1, 0) * SUB, SUB)
        below = pl.multiple_of(jnp.minimum(j + 1, blocks - 1) * SUB, SUB)
        top = (sub == 0) & (j == 0)
        bottom = (sub == SUB - 1) & (j == blocks - 1)
        near, far = near_ref[pl.ds(y, SUB), :], far_ref[pl.ds(y, SUB), :]
        low, high = jnp.where(even, far, near), jnp.where(even, near, far)
        tiles = [field_ref[pl.ds(x * wide + y, SUB), :] for x in range(rows)]
        edge = []
        for x, here in enumerate(tiles):
            spot = pl.ds(x * wide + y, SUB)
            over = field_ref[pl.ds(x * wide + above, SUB), :]
            under = field_ref[pl.ds(x * wide + below, SUB), :]
            beside = (low if x == 0 else tiles[x - 1]) + (high if x == rows - 1 else tiles[x + 1])
            ahead = pltpu.roll(jnp.where(sub == SUB - 1, over, here), 1, 0)
            behind = pltpu.roll(jnp.where(sub == 0, under, here), SUB - 1, 0)
            beside = beside + jnp.where(top, 0.0, ahead)
            beside = beside + jnp.where(bottom, 0.0, behind)
            beside = beside + jnp.where(lane == 0, 0.0, pltpu.roll(here, 1, 1))
            beside = beside + jnp.where(lane == depth - 1, 0.0, pltpu.roll(here, depth - 1, 1))
            rhs = rhs_ref[spot, :]
            at = (x * blocks + j) * across
            if grids:
                parts = []
                for t in range(across):
                    part = grids[0][at + t]
                    for grid in grids[1:]:
                        part = part + grid[at + t]
                    parts.append(part)
                rhs = rhs + jnp.concatenate(parts, axis=1)
                source_ref[spot, :] = rhs
            new = (1.0 - OMEGA) * here + (rhs + beside) * scale_ref[spot, :]
            out_ref[spot, :] = new
            if closing:
                for t in range(across):
                    to = pl.ds(pl.multiple_of((at + t) * SUB, SUB), SUB)
                    flat_ref[to, :] = new[:, t * LANES : (t + 1) * LANES]
            if x in (0, rows - 1):
                edge.append(new)
        if sending:
            sends[0][pl.ds(y, SUB), :] = jnp.where(even, edge[1], edge[0])
            sends[1][pl.ds(y, SUB), :] = jnp.where(even, edge[0], edge[1])

    def step(j, carry):
        for k in range(unroll):
            block(j * unroll + k)
        return carry

    lax.fori_loop(0, blocks // unroll, step, 0)
    if closing:
        gather_cells(most, code_ref, flat_ref, extra_ref, sampled_ref, lines_ref)


def stencil(field, stiff, layers, edge=None):
    sub = iota(field[0].shape, 0)
    turns = field[0].shape[1]
    out = []
    for index, here in enumerate(field):
        layer = index % layers
        before, after = pltpu.roll(here, 1, 0), pltpu.roll(here, SUB - 1, 0)
        if edge is not None:
            before = jnp.where(sub == 0, edge[index][0], before)
            after = jnp.where(sub == SUB - 1, edge[index][1], after)
        beside = before + after + pltpu.roll(here, 1, 1) + pltpu.roll(here, turns - 1, 1)
        if layer > 0:
            beside = beside + field[index - 1]
        if layer < layers - 1:
            beside = beside + field[index + 1]
        out.append((6.0 + stiff[layer]) * here - beside)
    return out


def inner(left, right, own):
    total = jnp.zeros_like(left[0])
    for a, b in zip(left, right):
        total = total + a * b
    return jnp.sum(jnp.where(own, total, 0.0), keepdims=True)


def wall_parts(force, stiff, layers, valid, own, force_ref, image_ref, twice_ref):
    force = [jnp.where(valid, tile, 0.0) for tile in force]
    image = [jnp.where(valid, tile, 0.0) for tile in stencil(force, stiff, layers)]
    twice = stencil(image, stiff, layers)
    for index in range(len(force)):
        force_ref[index] = force[index]
        image_ref[index] = image[index]
        twice_ref[index] = twice[index]
    return inner(force, force, own), inner(force, image, own)


def row_masks(me, devices, rows, shape):
    lead = (SUB - rows) // 2
    sub = iota(shape, 0)
    valid = ((sub >= lead) | (me > 0)) & ((sub < lead + rows) | (me < devices - 1))
    own = (sub >= lead) & (sub < lead + rows)
    return valid, own


def two_lanes(first, second, lanes):
    lane = iota((1, lanes), 1)
    return jnp.where(lane == 0, first, jnp.where(lane == 1, second, 0.0))


def pack_kernel(layers, rows, me_ref, start_ref, load_ref, stiff_ref, state_ref, near_ref, far_ref, own_ref):
    even = (me_ref[0] & 1) == 0
    turns = start_ref.shape[3]
    lead = (SUB - rows) // 2
    tiles = 3 * layers
    for c in range(3):
        for s in range(rows):
            own_ref[c, s : s + 1, :] = state_ref[3 + c : 4 + c, s * turns : (s + 1) * turns]
    at = 0
    near_ref[...] = jnp.zeros_like(near_ref)
    far_ref[...] = jnp.zeros_like(far_ref)
    for kind, count in enumerate((tiles, tiles, layers, 3)):
        deep = lead + 1 if kind == 0 else lead
        for i in range(count):
            if kind == 0:
                tile = start_ref[i // layers, i % layers]
            elif kind == 1:
                tile = load_ref[i // layers, i % layers]
            else:
                tile = stiff_ref[i] if kind == 2 else own_ref[i]
            first, last = tile[0:deep, :], tile[rows - deep : rows, :]
            near_ref[at : at + deep, :] = jnp.where(even, last, first)
            far_ref[at : at + deep, :] = jnp.where(even, first, last)
            at += deep


def wall_first_kernel(devices, layers, me_ref, start_ref, load_ref, stiff_in_ref, state_ref, near_ref, far_ref, past_ref,
                      send_ref, base_ref, stiff_ref, force_ref, image_ref, twice_ref, wide_ref):
    rows, turns = start_ref.shape[2:]
    lead = (SUB - rows) // 2
    tiles = 3 * layers
    even = (me_ref[0] & 1) == 0
    edge, at = [], 0
    for kind, count in enumerate((tiles, tiles, layers, 3)):
        deep = lead + 1 if kind == 0 else lead
        for i in range(count):
            near, far = near_ref[at : at + deep, :], far_ref[at : at + deep, :]
            low, high = jnp.where(even, far, near), jnp.where(even, near, far)
            to = (0, tiles, 2 * tiles, 2 * tiles + layers)[kind] + i
            wide_ref[to, 0:lead, :] = low[deep - lead : deep, :]
            wide_ref[to, lead + rows : SUB, :] = high[0:lead, :]
            if kind == 0:
                edge.append((low[0:1, :], high[lead:deep, :]))
                wide_ref[to, lead : lead + rows, :] = start_ref[i // layers, i % layers]
            elif kind == 1:
                wide_ref[to, lead : lead + rows, :] = load_ref[i // layers, i % layers]
            elif kind == 2:
                wide_ref[to, lead : lead + rows, :] = stiff_in_ref[i]
            else:
                for s in range(rows):
                    wide_ref[to, lead + s : lead + s + 1, :] = state_ref[3 + i : 4 + i, s * turns : (s + 1) * turns]
            at += deep
    start = [wide_ref[i] for i in range(tiles)]
    stiff = [wide_ref[2 * tiles + i] for i in range(layers)]
    for i in range(layers):
        stiff_ref[i] = stiff[i]
    applied = stencil(start, stiff, layers, edge)
    for i in range(tiles):
        base_ref[i] = wide_ref[tiles + i] - applied[i]
    valid, own = row_masks(me_ref[0], devices, rows, (SUB, turns))
    force = [base_ref[i] for i in range(tiles)]
    for c in range(3):
        force[c * layers] = force[c * layers] + wide_ref[2 * tiles + layers + c]
    square, product = wall_parts(force, stiff, layers, valid, own, force_ref, image_ref, twice_ref)
    history = past_ref.shape[1]
    gram = jnp.zeros((history, history), F32)
    for c in range(past_ref.shape[0]):
        gram = gram + dot(past_ref[c], past_ref[c], ((1,), (1,)))
    send_ref[...] = jnp.broadcast_to(two_lanes(square, product, LANES), (devices, LANES))
    chunk = history * history // devices
    for d in range(devices):
        row, left = d * chunk // history, d * chunk % history
        send_ref[d : d + 1, 2 : 2 + chunk] = gram[row : row + 1, left : left + chunk]


def wall_next_kernel(devices, layers, rows, me_ref, near_ref, far_ref, state_ref, base_ref, stiff_ref,
                     send_ref, force_ref, image_ref, twice_ref, pull_ref):
    tiles, _, turns = base_ref.shape
    lead = (SUB - rows) // 2
    me = me_ref[0]
    even = (me & 1) == 0
    for c in range(3):
        near, far = near_ref[c : c + 1, :], far_ref[c : c + 1, :]
        low, high = jnp.where(even, far, near), jnp.where(even, near, far)
        for s in range(rows):
            pull_ref[c, lead + s : lead + s + 1, :] = state_ref[3 + c : 4 + c, s * turns : (s + 1) * turns]
        for s in range(lead):
            pull_ref[c, s : s + 1, :] = low[:, s * turns : (s + 1) * turns]
            pull_ref[c, lead + rows + s : lead + rows + s + 1, :] = high[:, s * turns : (s + 1) * turns]
    valid, own = row_masks(me, devices, rows, (SUB, turns))
    force = [base_ref[i] for i in range(tiles)]
    for c in range(3):
        force[c * layers] = force[c * layers] + pull_ref[c]
    stiff = [stiff_ref[i] for i in range(layers)]
    square, product = wall_parts(force, stiff, layers, valid, own, force_ref, image_ref, twice_ref)
    send_ref[...] = jnp.broadcast_to(two_lanes(square, product, LANES), (devices, LANES))


def summed(got_ref):
    return jnp.sum(got_ref[...], axis=0, keepdims=True)


def wall_second_kernel(rows, got_ref, force_ref, image_ref, twice_ref, send_ref):
    total = summed(got_ref)
    alpha = total[:, 0:1] / total[:, 1:2]
    shape = force_ref.shape[1:]
    lead = (SUB - rows) // 2
    sub = iota(shape, 0)
    own = (sub >= lead) & (sub < lead + rows)
    square = jnp.zeros(shape, F32)
    product = jnp.zeros(shape, F32)
    for i in range(force_ref.shape[0]):
        residual = force_ref[i] - alpha * image_ref[i]
        image = image_ref[i] - alpha * twice_ref[i]
        square = square + residual * residual
        product = product + residual * image
    square = jnp.sum(jnp.where(own, square, 0.0), keepdims=True)
    product = jnp.sum(jnp.where(own, product, 0.0), keepdims=True)
    lane = iota((1, LANES), 1)
    row = jnp.where(lane == 0, square, jnp.where(lane == 1, product, total))
    send_ref[...] = jnp.broadcast_to(row, send_ref.shape)


def wall_last_kernel(layers, rows, at, one_ref, two_ref, force_ref, image_ref, start_ref, wall_ref, solid_ref):
    one = summed(one_ref)
    two = jnp.sum(two_ref[:, at : at + 2], axis=0, keepdims=True)
    norm, alpha = one[:, 0:1], one[:, 0:1] / one[:, 1:2]
    newer = two[:, 0:1]
    ratio = newer / norm
    beta = newer / (two[:, 1:2] - ratio * newer / alpha)
    turns = force_ref.shape[2]
    lead = (SUB - rows) // 2
    for i in range(force_ref.shape[0]):
        c, layer = i // layers, i % layers
        force = force_ref[i]
        residual = force - alpha * image_ref[i]
        moved = alpha * force + beta * (residual + ratio * force)
        wall = start_ref[c, layer] + moved[lead : lead + rows, :]
        wall_ref[c, layer] = wall
        if layer == 0:
            for s in range(rows):
                solid_ref[c : c + 1, s * turns : (s + 1) * turns] = wall[s : s + 1, :]


def returned_kernel(devices, most, turn, got_ref, owner_ref, rank_ref, normals_ref, state_ref, solid_ref, past_ref, *rest):
    if turn == 0:
        output_ref, resid_ref, send_ref = rest
    else:
        last_ref, output_ref, resid_ref, send_ref = rest
    named, placed = onehots(owner_ref[...], rank_ref[...], devices, most)
    spread = dot(got_ref[:, 0:most], named, ((0,), (0,)))
    sampled = jnp.sum(spread * placed, axis=0, keepdims=True)
    output_ref[0:3, :] = solid_ref[...]
    output_ref[3:6, :] = -sampled * normals_ref[...]
    resid_ref[...] = output_ref[...] - state_ref[...]
    history = past_ref.shape[1]
    points = state_ref.shape[1]
    sub = iota((SUB, points), 0)
    parts = jnp.zeros((SUB, history), F32)
    newest = jnp.zeros((SUB, SUB), F32)
    for c in range(6):
        resid = resid_ref[c : c + 1, :]
        pair = jnp.where(sub == 0, resid, 0.0)
        if turn > 0:
            pair = jnp.where(sub == 1, resid - last_ref[c : c + 1, :], pair)
            newest = newest + dot(pair, pair, ((1,), (1,)))
        parts = parts + dot(pair, past_ref[c], ((1,), (1,)))
    send_ref[...] = jnp.zeros_like(send_ref)
    send_ref[:, 0:history] = jnp.broadcast_to(parts[0:1, :], (devices, history))
    if turn > 0:
        send_ref[:, history : 2 * history] = jnp.broadcast_to(parts[1:2, :], (devices, history))
        send_ref[:, 2 * history : 2 * history + 2] = jnp.broadcast_to(newest[1:2, 0:2], (devices, 2))


def gram_of(gram_ref, history, work_ref):
    devices = gram_ref.shape[0]
    chunk = history * history // devices
    for d in range(devices):
        row, left = d * chunk // history, d * chunk % history
        work_ref[row : row + 1, left : left + chunk] = gram_ref[d : d + 1, 2 : 2 + chunk]


def eliminated(table, history):
    sub, lane = iota(table.shape, 0), iota(table.shape, 1)
    diagonal = (sub == lane) & (sub < history)
    trace = jnp.sum(jnp.where(diagonal, table, 0.0), keepdims=True)
    ridge = RIDGE * trace / history + TINY
    table = jnp.where(diagonal, table + ridge, table)
    table = jnp.where((lane == sub + history) & (sub < history), 1.0, table)
    for k in range(0, history, 2):
        first, second = table[k : k + 1, :], table[k + 1 : k + 2, :]
        top, cross, low = first[:, k : k + 1], first[:, k + 1 : k + 2], second[:, k + 1 : k + 2]
        scale = 1.0 / (top * low - cross * cross)
        left = jnp.where(sub[:, 0:1] > k + 1, table[:, k : k + 1], 0.0)
        right = jnp.where(sub[:, 0:1] > k + 1, table[:, k + 1 : k + 2], 0.0)
        table = table - left * ((low * first - cross * second) * scale) - right * ((top * second - cross * first) * scale)
    return table[history:, history : 2 * history]


def inverse_kernel(history, gram_ref, out_ref, work_ref):
    work_ref[...] = jnp.zeros_like(work_ref)
    gram_of(gram_ref, history, work_ref)
    sub, lane = iota(work_ref.shape, 0), iota(work_ref.shape, 1)
    table = jnp.where((sub == lane + history) & (lane < history), 1.0, work_ref[...])
    out_ref[...] = eliminated(table, history)


def coefficients(history, got_ref, gram_ref, work_ref):
    total = summed(got_ref)
    work_ref[...] = jnp.zeros_like(work_ref)
    gram_of(gram_ref, history, work_ref)
    sub, lane = iota(work_ref.shape, 0), iota(work_ref.shape, 1)
    swap = history - 1
    fresh = total[:, history : 2 * history]
    square = total[:, 2 * history + 1 : 2 * history + 2]
    along = total[:, 2 * history : 2 * history + 1]
    edge = iota((1, history), 1) == swap
    work_ref[swap : swap + 1, 0:history] = jnp.where(edge, square, fresh)
    work_ref[history : history + 1, 0:history] = jnp.where(edge, along, total[:, 0:history])
    line = work_ref[swap : swap + 1, :]
    column = jnp.sum(jnp.where(sub == lane, line, 0.0), axis=1, keepdims=True)
    table = jnp.where((lane == swap) & (sub < history), column, work_ref[...])
    return eliminated(table, history)[0:1]


def update_kernel(devices, most, lead, turns, me_ref, got_ref, inverse_ref, output_ref, past_ref, owner_ref, rank_ref, normals_ref,
                  next_ref, send_ref, near_ref, far_ref):
    history = past_ref.shape[1]
    total = summed(got_ref)
    rows = dot(jnp.broadcast_to(total[:, 0:history], (SUB, history)), inverse_ref[...], ((1,), (0,)))
    for c in range(6):
        next_ref[c : c + 1, :] = output_ref[c : c + 1, :] + dot(rows, past_ref[c], ((1,), (0,)))[0:1, :]
    me = me_ref[0]
    points = output_ref.shape[1]
    named, placed = onehots(owner_ref[...], rank_ref[...], devices, most)
    flux = flux_of(normals_ref[...], next_ref[...])
    send_ref[...] = jnp.zeros_like(send_ref)
    send_ref[:, 0:most] = dot(named, placed * flux, ((1,), (1,)))
    half = lead * turns
    even = (me & 1) == 0
    for c in range(3):
        first, last = next_ref[3 + c : 4 + c, 0:half], next_ref[3 + c : 4 + c, points - half : points]
        near_ref[c : c + 1, :] = jnp.where(even, last, first)
        far_ref[c : c + 1, :] = jnp.where(even, first, last)


def finish_kernel(got_ref, gram_ref, output_ref, past_ref, last_ref, next_ref, work_ref):
    history = past_ref.shape[1]
    coeffs = coefficients(history, got_ref, gram_ref, work_ref)
    swap = history - 1
    newest = coeffs[:, swap:history]
    rows = jnp.broadcast_to(coeffs, (SUB, history))
    rows = jnp.where(iota(rows.shape, 1) == swap, 0.0, rows)
    for c in range(6):
        here = output_ref[c : c + 1, :]
        moved = dot(rows, past_ref[c], ((1,), (0,)))[0:1, :]
        next_ref[c : c + 1, :] = here + moved + newest * (here - last_ref[c : c + 1, :])


def local(
    pressure_start,
    fluid_coef,
    fluid_rhs,
    wall_start,
    wall_stiff,
    wall_load,
    normals,
    fluid_owner,
    fluid_cell,
    interface_start,
    past_residual,
    past_output,
):
    devices = lax.axis_size(AXES)
    me = lax.axis_index(AXES).astype(jnp.int32).reshape(1)
    rows, wide, depth = pressure_start.shape
    points = fluid_cell.shape[0]
    most = max(2, 2 * points // devices)
    history = past_residual.shape[0]
    layers, wall_rows, turns = wall_stiff.shape
    flat = (rows * wide, depth)
    plane = (wide, depth)
    lead = (SUB - wall_rows) // 2
    tiles = 3 * layers
    tile = (tiles, SUB, turns)
    slots = LANES * -(-2 * most // LANES)

    owner = fluid_owner.reshape(1, points)
    field = pressure_start.reshape(flat)
    low, high = field[0:wide], field[flat[0] - wide :]
    even = (me[0] & 1) == 0
    ends = tie(jnp.where(even, high, low), jnp.where(even, low, high))
    near, far = swap(*ends)
    past_r = jnp.transpose(past_residual, (1, 0, 2))
    past_w = jnp.transpose(past_output, (1, 0, 2))
    rhs = fluid_rhs.reshape(flat)

    owner, _ = tie(owner, ends)
    send, rank = call(
        functools.partial(route_kernel, devices, most),
        [((devices, slots), F32), ((1, points), jnp.int32)],
        [vmem()] * 4, limit=4,
    )(owner, fluid_cell.reshape(1, points), normals, interface_start)
    got = exchange(send)
    got, coef, start_in, load_in, state = tie(got, fluid_coef, wall_start, wall_load, interface_start)
    cells = tiled_place(jnp.maximum(got[:, 0:most].astype(jnp.int32) - 1, 0), depth)
    flux, spot = got, most
    scale = (OMEGA / (6.0 + coef)).reshape(flat)

    needed = (3 * (lead + 1) + 3 * lead + lead) * layers + 3 * lead
    packed = (SUB * -(-needed // SUB), turns)
    packs = call(
        functools.partial(pack_kernel, layers, wall_rows),
        [(packed, F32)] * 2, [smem()] + [vmem()] * 4, [pltpu.VMEM((3, wall_rows, turns), F32)], limit=2,
    )(me, start_in, load_in, wall_stiff, state)

    small = ((devices, LANES), F32)
    padded = LANES * -(-2 * history // LANES)
    output = resid = wall = None
    for turn in range(COUPLE):
        for sweep in range(SWEEPS):
            last = sweep + 1 == SWEEPS
            sending = not last or turn + 1 < COUPLE
            opening, closing = sweep == 0, not sending
            carrying = turn > 0
            extra_in, extra_spec, extra_out, scratch = [], [], [], []
            if opening:
                extra_in, extra_spec = [cells, flux], [smem(), smem()]
                extra_out = [(flat, F32)]
                scratch = [pltpu.VMEM((flat[0] * depth // (SUB * LANES), SUB, LANES), F32)] * GRIDS
            if closing:
                extra_in, extra_spec = [cells], [smem()]
                if carrying:
                    sums = call(
                        functools.partial(wall_second_kernel, wall_rows),
                        [((SUB, LANES), F32)], [vmem()] * 4, limit=2,
                    )(one, force, image, twice)[0]
                    extra_in, extra_spec = [cells, sums], [smem(), vmem()]
                extra_out = [((devices, LANES * -(-(most + 2) // LANES)), F32)]
                scratch = [pltpu.VMEM((devices * most, LANES), F32), pltpu.VMEM((flat[0] * depth // LANES, LANES), F32)]
            field, *rest = call(
                functools.partial(sweep_kernel, rows, most, spot, opening, closing, sending, carrying),
                [(flat, F32)] + [(plane, F32)] * (2 if sending else 0) + extra_out,
                [smem()] + [vmem()] * 5 + extra_spec, scratch, limit=26 if opening else 12,
            )(me, field, near, far, rhs if opening else source, scale, *extra_in)
            if sending:
                ends, rest = rest[:2], rest[2:]
            if opening:
                source = rest[0]
            if closing:
                sampled = rest[0]
            elif last:
                near, far = swap(*ends)
                sampled = call(
                    functools.partial(gather_kernel, most),
                    [((devices, LANES * -(-most // LANES)), F32)],
                    [smem(), vmem()],
                    [pltpu.VMEM((devices * most, LANES), F32), pltpu.VMEM((flat[0] * depth // LANES, LANES), F32)],
                    limit=12,
                )(cells, field)[0]
            else:
                near, far = swap(*ends)
            if turn == 0 and sweep == 0:
                packs, _ = tie(packs, ends)
                pack_near, pack_far = swap(*packs)
                far, pack_far = tie(far, pack_far)
            if turn == 0 and sweep == 1:
                pack_near, ends = tie(pack_near, ends)
                sums, base, stiff, force, image, twice = call(
                    functools.partial(wall_first_kernel, devices, layers),
                    [small, (tile, F32), ((layers, SUB, turns), F32)] + [(tile, F32)] * 3,
                    [smem()] + [vmem()] * 7,
                    [pltpu.VMEM((2 * tiles + layers + 3, SUB, turns), F32)], limit=6,
                )(me, start_in, load_in, wall_stiff, state, pack_near, pack_far, past_r)
                one = exchange(sums)
                one, far = tie(one, far)
            if turn == 0 and sweep == 2:
                one, ends = tie(one, ends)
                sums = call(
                    functools.partial(wall_second_kernel, wall_rows),
                    [small], [vmem()] * 4, limit=2,
                )(one, force, image, twice)[0]
                two = exchange(sums)
                inverse = call(
                    functools.partial(inverse_kernel, history),
                    [((history, history), F32)], [vmem()], [pltpu.VMEM((2 * history, padded), F32)], limit=2,
                )(two)[0]
                wall, solid = call(
                    functools.partial(wall_last_kernel, layers, wall_rows, 0),
                    [(wall_start.shape, F32), ((3, points), F32)], [vmem()] * 5, limit=2,
                )(one, two, force, image, wall_start)
                inverse, far, solid = tie(inverse, far, solid)
                grams = two
            if turn == 1 and sweep == 0:
                pulls, ends = tie(pulls, ends)
                pull_near, pull_far = swap(*pulls)
                far, pull_far = tie(far, pull_far)
            if turn == 1 and sweep == 1:
                pull_near, ends = tie(pull_near, ends)
                sums, force, image, twice = call(
                    functools.partial(wall_next_kernel, devices, layers, wall_rows),
                    [small, (tile, F32), (tile, F32), (tile, F32)],
                    [smem()] + [vmem()] * 5,
                    [pltpu.VMEM((3, SUB, turns), F32)], limit=2,
                )(me, pull_near, pull_far, state, base, stiff)
                one = exchange(sums)
                one, far = tie(one, far)
        back = exchange(sampled)
        if turn + 1 == COUPLE:
            wall, solid = call(
                functools.partial(wall_last_kernel, layers, wall_rows, most),
                [(wall_start.shape, F32), ((3, points), F32)], [vmem()] * 5, limit=2,
            )(one, back, force, image, wall_start)
        last_args = () if turn == 0 else (resid,)
        before = output
        output, resid, sums = call(
            functools.partial(returned_kernel, devices, most, turn),
            [((6, points), F32), ((6, points), F32), ((devices, LANES * -(-(2 * history + 2) // LANES)), F32)],
            [vmem()] * (7 + len(last_args)), limit=4,
        )(back, owner, rank, normals, state, solid, past_r, *last_args)
        if turn + 1 < COUPLE:
            sums, inverse = tie(sums, inverse)
        total = exchange(sums)
        if turn + 1 < COUPLE:
            state, flux, *pulls = call(
                functools.partial(update_kernel, devices, most, lead, turns),
                [((6, points), F32), ((devices, LANES * -(-most // LANES)), F32)] + [((3, lead * turns), F32)] * 2,
                [smem()] + [vmem()] * 7, limit=4,
            )(me, total, inverse, output, past_w, owner, rank, normals)
            flux, spot = exchange(flux), 0
            flux, pulls = tie(flux, pulls)
        else:
            work = [pltpu.VMEM((SUB * -(-(history + 1) // SUB), padded), F32)]
            state = call(
                finish_kernel, [((6, points), F32)], [vmem()] * 5, work, limit=4,
            )(total, grams, output, past_w, before)[0]
    return (state, field.reshape(pressure_start.shape), wall)


def solution(mesh):
    placed = (
        P(("solver", "space"), None, None),
        P(("solver", "space"), None, None),
        P(("solver", "space"), None, None),
        P(None, None, ("solver", "space"), None),
        P(None, ("solver", "space"), None),
        P(None, None, ("solver", "space"), None),
        P(None, ("solver", "space")),
        P(("solver", "space"), None),
        P(("solver", "space")),
        P(None, ("solver", "space")),
        P(None, None, ("solver", "space")),
        P(None, None, ("solver", "space")),
    )

    return jax.shard_map(
        local,
        mesh=mesh,
        in_specs=placed,
        out_specs=(
            P(None, ("solver", "space")),
            P(("solver", "space"), None, None),
            P(None, None, ("solver", "space"), None),
        ),
        check_vma=False,
    )
```

profile of v0, /device:TPU:0, one launch (start us, length us, event | category | flops | bytes accessed | tf_op | source)
XLA Modules:
  0.0 240.8 jit_solution(570494823654582195)
XLA Ops:
  0.7 2.4 %select_bitcast_fusion = (f32[256,512]{1,0:T(8,128)}, f32[256,512]{1,0:T(8,128)}) fusion(f32[4,256,512]{2,1,0:T(8,128)} %param.12, pred[]{:T(512)S(6)} %eq.7), kind=kLoop, calls=%fused_computation.1 | loop fusion | flops 262144 | bytes 2097153 | tf_op jit(solution)/shard_map/jit(_where)/select_n | solution.py:603
  3.1 1.4 shard_map.139
  4.6 7.3 %all-to-all-start = ((f32[32,1,128]{2,1,0:T(1,128)}), f32[32,1,128]{2,1,0:T(1,128)S(1)}, u32[]{:S(2)}, u32[]{:S(2)}) async-start(f32[32,1,128]{2,1,0:T(1,128)} %bitcast.8), calls=%async_computation | async-start | bytes 32768 | tf_op jit(solution)/shard_map/all_to_all | solution.py:55
  11.9 0.3 collective-permute-start
  12.2 0.7 collective-permute-start.1
  12.9 6.1 %all-to-all-done = f32[32,1,128]{2,1,0:T(1,128)S(1)} async-done(((f32[32,1,128]{2,1,0:T(1,128)}), f32[32,1,128]{2,1,0:T(1,128)S(1)}, u32[]{:S(2)}, u32[]{:S(2)}) %all-to-all-start) | async-done | bytes 16416 | tf_op jit(solution)/shard_map/all_to_all | solution.py:55
  19.0 0.1 fusion.5.refs_6_.code_ref
  19.1 0.0 copy-start
  19.1 0.0 copy-start.2
  19.1 0.3 add_divide_fusion
  19.4 1.3 copy-done
  20.7 0.6 copy-done.2
  21.3 8.5 %shard_map.140 = (f32[1024,512]{1,0:T(8,128)S(1)}, f32[256,512]{1,0:T(8,128)S(1)}, f32[256,512]{1,0:T(8,128)S(1)}, f32[1024,512]{1,0:T(8,128)S(1)}) custom-call(s32[1]{0:T(128)} %bitcast.refs_0_.me_ref, f32[1024,512]{1,0:T(8,128)S(1)} %bitcast.62, f32[256,512]{1,0:T(8,128)S(1)} %collective-permute-done.refs_2_, ...), custom_call_target="tpu_custom_call" | custom-call | tf_op jit(solution)/shard_map/pallas_call | solution.py:652
  29.8 0.7 collective-permute-start.3
  30.5 6.4 %collective-permute-start.2 = (f32[256,512]{1,0:T(8,128)S(1)}, f32[256,512]{1,0:T(8,128)S(1)}, u32[]{:S(2)}, u32[]{:S(2)}) collective-permute-start(f32[256,512]{1,0:T(8,128)S(1)} %get-tuple-element.92), channel_id=1, source_target_pairs={{0,1},{1,0},{2,3},{3,2},{4,5},{5,4},{6,7},{7,6},{8,9},{9,8},{10,11... | collective-permute-start | bytes 1572872 | tf_op jit(solution)/shard_map/ppermute | solution.py:71
  36.9 0.1 shard_map.141
  37.0 0.7 collective-permute-start.4
  37.7 0.7 collective-permute-done.2.refs_2_
  38.4 2.3 shard_map.142
  40.7 0.7 collective-permute-start.7
  41.4 9.9 %collective-permute-start.5 = (f32[256,512]{1,0:T(8,128)S(1)}, f32[256,512]{1,0:T(8,128)S(1)}, u32[]{:S(2)}, u32[]{:S(2)}) collective-permute-start(f32[256,512]{1,0:T(8,128)S(1)} %get-tuple-element.103), channel_id=1, source_target_pairs={{0,1},{1,0},{2,3},{3,2},{4,5},{5,4},{6,7},{7,6},{8,9},{9,8},{10,11... | collective-permute-start | bytes 1572872 | tf_op jit(solution)/shard_map/ppermute | solution.py:71
  51.3 0.1 collective-permute-start.6
  51.4 1.7 collective-permute-done.6.near_ref
  53.0 1.0 shard_map.143
  54.1 25.6 %all_to_all.103 = f32[32,1,128]{2,1,0:T(1,128)S(1)} all-to-all(f32[32,1,128]{2,1,0:T(1,128)S(1)} %bitcast.87), channel_id=1, replica_groups=mesh['solver'=4,'space'=8] {'solver','space'}, dimensions={0} | all-to-all | bytes 32768 | tf_op jit(solution)/shard_map/all_to_all | solution.py:55
  79.7 2.3 shard_map.144
  82.0 0.7 collective-permute-start.9
  82.7 1.9 collective-permute-start.8
  84.6 0.3 shard_map.145
  84.9 13.5 %all_to_all.104 = f32[32,1,128]{2,1,0:T(1,128)S(1)} all-to-all(f32[32,1,128]{2,1,0:T(1,128)S(1)} %bitcast.85), channel_id=1, replica_groups=mesh['solver'=4,'space'=8] {'solver','space'}, dimensions={0} | all-to-all | bytes 32768 | tf_op jit(solution)/shard_map/all_to_all | solution.py:55
  98.4 1.0 shard_map.147
  99.4 2.8 %shard_map.146.inverse_ref = f32[32,32]{1,0:T(8,128)S(1)} custom-call(f32[32,128]{1,0:T(8,128)S(1)} %bitcast.66), custom_call_target="tpu_custom_call" | custom-call | tf_op jit(solution)/shard_map/pallas_call | solution.py:695
  102.2 2.3 shard_map.148
  104.5 0.1 collective-permute-start.10
  104.6 0.8 collective-permute-start.11
  105.4 5.2 %shard_map.149 = f32[32,128]{1,0:T(8,128)S(1)} custom-call(s32[32,64]{1,0:T(8,128)S(1)} %fusion.5.refs_6_.code_ref, f32[1024,512]{1,0:T(8,128)S(1)} %get-tuple-element.120.field_ref.refs_1_), custom_call_target="tpu_custom_call" | custom-call | tf_op jit(solution)/shard_map/pallas_call | solution.py:665
  110.6 13.9 %all_to_all.105 = f32[32,1,128]{2,1,0:T(1,128)S(1)} all-to-all(f32[32,1,128]{2,1,0:T(1,128)S(1)} %bitcast.82), channel_id=1, replica_groups=mesh['solver'=4,'space'=8] {'solver','space'}, dimensions={0} | all-to-all | bytes 32768 | tf_op jit(solution)/shard_map/all_to_all | solution.py:55
  124.5 1.5 shard_map.150
  126.0 8.9 %all_to_all.106 = f32[32,1,128]{2,1,0:T(1,128)S(1)} all-to-all(f32[32,1,128]{2,1,0:T(1,128)S(1)} %bitcast.91), channel_id=1, replica_groups=mesh['solver'=4,'space'=8] {'solver','space'}, dimensions={0} | all-to-all | bytes 32768 | tf_op jit(solution)/shard_map/all_to_all | solution.py:55
  134.9 1.1 shard_map.151
  135.9 8.9 %all_to_all.107 = f32[32,1,128]{2,1,0:T(1,128)S(1)} all-to-all(f32[32,1,128]{2,1,0:T(1,128)S(1)} %bitcast.90), channel_id=1, replica_groups=mesh['solver'=4,'space'=8] {'solver','space'}, dimensions={0} | all-to-all | bytes 32768 | tf_op jit(solution)/shard_map/all_to_all | solution.py:55
  144.8 8.4 %shard_map.152 = (f32[1024,512]{1,0:T(8,128)S(1)}, f32[256,512]{1,0:T(8,128)S(1)}, f32[256,512]{1,0:T(8,128)S(1)}, f32[1024,512]{1,0:T(8,128)S(1)}) custom-call(s32[1]{0:T(128)} %bitcast.refs_0_.me_ref, f32[1024,512]{1,0:T(8,128)S(1)} %get-tuple-element.120.field_ref.refs_1_, f32[256,512]{1,0:T(8,128)S(1)} %collective-permute-done.10.refs_2_, ...), custom_call_target="tpu_custom_call" | custom-call | tf_op jit(solution)/shard_map/pallas_call | solution.py:652
  153.2 0.7 collective-permute-start.13
  153.9 1.8 collective-permute-start.12
  155.7 0.6 collective-permute-start.14
  156.4 0.9 collective-permute-done.12.refs_2_
  157.3 2.3 shard_map.153
  159.5 0.7 collective-permute-start.17
  160.2 13.4 %collective-permute-start.15 = (f32[256,512]{1,0:T(8,128)S(1)}, f32[256,512]{1,0:T(8,128)S(1)}, u32[]{:S(2)}, u32[]{:S(2)}) collective-permute-start(f32[256,512]{1,0:T(8,128)S(1)} %get-tuple-element.143), channel_id=1, source_target_pairs={{0,1},{1,0},{2,3},{3,2},{4,5},{5,4},{6,7},{7,6},{8,9},{9,8},{10,11... | collective-permute-start | bytes 1572872 | tf_op jit(solution)/shard_map/ppermute | solution.py:71
  173.7 0.1 collective-permute-start.16
  173.7 1.5 collective-permute-done.16.near_ref
  175.2 0.3 shard_map.154
  175.6 13.2 %all_to_all.108 = f32[32,1,128]{2,1,0:T(1,128)S(1)} all-to-all(f32[32,1,128]{2,1,0:T(1,128)S(1)} %bitcast.88), channel_id=1, replica_groups=mesh['solver'=4,'space'=8] {'solver','space'}, dimensions={0} | all-to-all | bytes 32768 | tf_op jit(solution)/shard_map/all_to_all | solution.py:55
  188.8 2.3 shard_map.155
  191.1 0.1 collective-permute-start.18
  191.2 0.9 collective-permute-start.19
  192.1 0.3 shard_map.156.refs_7_
  192.4 0.7 collective-permute-done.18.refs_2_
  193.1 7.2 %shard_map.157 = (f32[1024,512]{1,0:T(8,128)}, f32[32,128]{1,0:T(8,128)S(1)}) custom-call(s32[1]{0:T(128)} %bitcast.refs_0_.me_ref, f32[1024,512]{1,0:T(8,128)S(1)} %get-tuple-element.153.refs_1_, f32[256,512]{1,0:T(8,128)S(1)} %collective-permute-done.18.refs_2_, f32[256,512]{1,0:T(8,128)S(1)} %collective-permute-done.19.refs_3_, ...), custom_call_target="tpu_custom_call" | custom-call | tf_op jit(solution)/shard_map/pallas_call | solution.py:652
  200.3 24.6 %all_to_all.109 = f32[32,1,128]{2,1,0:T(1,128)S(1)} all-to-all(f32[32,1,128]{2,1,0:T(1,128)S(1)} %bitcast.86), channel_id=1, replica_groups=mesh['solver'=4,'space'=8] {'solver','space'}, dimensions={0} | all-to-all | bytes 32768 | tf_op jit(solution)/shard_map/all_to_all | solution.py:55
  224.9 1.1 shard_map.158
  226.0 1.9 shard_map.159
  227.9 8.9 %all_to_all.110 = f32[32,1,128]{2,1,0:T(1,128)S(1)} all-to-all(f32[32,1,128]{2,1,0:T(1,128)S(1)} %bitcast.89), channel_id=1, replica_groups=mesh['solver'=4,'space'=8] {'solver','space'}, dimensions={0} | all-to-all | bytes 32768 | tf_op jit(solution)/shard_map/all_to_all | solution.py:55
  236.7 4.0 %shard_map.160 = f32[6,1024]{1,0:T(8,128)} custom-call(f32[32,128]{1,0:T(8,128)S(1)} %bitcast.81, f32[32,128]{1,0:T(8,128)S(1)} %bitcast.67, f32[6,1024]{1,0:T(8,128)S(1)} %get-tuple-element.164.output_ref, f32[6,32,1024]{2,1,0:T(8,128)S(1)} %bitcast.64, f32[6,1024]{1,0:T(8,128)S(1)} %get-tuple-element.129.output_ref.last_ref), custom_call_target="tpu_custom_call" | custom-call | tf_op jit(solution)/shard_map/pallas_call | solution.py:745
  (35 shorter events, 0.1 us)
Async XLA Ops:
  0.6 2.5 %copy-start.9 = (s32[1024,1]{0,1:T(1,128)S(1)}, s32[1024,1]{0,1:T(1,128)}, u32[]{:S(2)}) copy-start(s32[1024,1]{0,1:T(1,128)} %param.19) | copy-start | bytes 12292
  0.6 2.5 %copy-start.7 = (f32[3,1024]{1,0:T(4,128)S(1)}, f32[3,1024]{1,0:T(4,128)}, u32[]{:S(2)}) copy-start(f32[3,1024]{1,0:T(4,128)} %normals_ref.7) | copy-start | bytes 36868
  0.7 2.5 %copy-start.5 = (f32[6,1024]{1,0:T(8,128)S(1)}, f32[6,1024]{1,0:T(8,128)}, u32[]{:S(2)}) copy-start(f32[6,1024]{1,0:T(8,128)} %state_ref.4) | copy-start | bytes 73732
  0.7 2.5 %copy-start.10 = (s32[1024]{0:T(1024)S(1)}, s32[1024]{0:T(1024)}, u32[]{:S(2)}) copy-start(s32[1024]{0:T(1024)} %param.20) | copy-start | bytes 12292
  0.7 18.4 %copy-start.11 = (f32[4,256,512]{2,1,0:T(8,128)S(1)}, f32[4,256,512]{2,1,0:T(8,128)}, u32[]{:S(2)}) copy-start(f32[4,256,512]{2,1,0:T(8,128)} %param.13) | copy-start | bytes 6291460
  4.6 14.4 %all-to-all-start = ((f32[32,1,128]{2,1,0:T(1,128)}), f32[32,1,128]{2,1,0:T(1,128)S(1)}, u32[]{:S(2)}, u32[]{:S(2)}) async-start(f32[32,1,128]{2,1,0:T(1,128)} %bitcast.8), calls=%async_computation | async-start | bytes 32768 | tf_op jit(solution)/shard_map/all_to_all | solution.py:55
  11.9 7.5 %collective-permute-start = (f32[256,512]{1,0:T(8,128)}, f32[256,512]{1,0:T(8,128)S(1)}, u32[]{:S(2)}, u32[]{:S(2)}) collective-permute-start(f32[256,512]{1,0:T(8,128)} %get-tuple-element.85), channel_id=1, source_target_pairs={{0,1},{1,0},{2,3},{3,2},{4,5},{5,4},{6,7},{7,6},{8,9},{9,8},{10,11... | collective-permute-start | bytes 1572872 | tf_op jit(solution)/shard_map/ppermute | solution.py:71
  12.2 7.2 %collective-permute-start.1 = (f32[256,512]{1,0:T(8,128)}, f32[256,512]{1,0:T(8,128)S(1)}, u32[]{:S(2)}, u32[]{:S(2)}) collective-permute-start(f32[256,512]{1,0:T(8,128)} %get-tuple-element.86), channel_id=1, source_target_pairs={{1,2},{3,4},{5,6},{7,8},{9,10},{11,12},{13,14},{15,16},{17,18},{19... | collective-permute-start | bytes 1572872 | tf_op jit(solution)/shard_map/ppermute | solution.py:71
  19.1 1.6 copy-start
  19.1 2.2 copy-start.2
  21.3 15.6 %copy-start.4 = (f32[3,8,4,256]{3,2,1,0:T(4,128)S(1)}, f32[3,8,4,256]{3,2,1,0:T(4,128)}, u32[]{:S(2)}) copy-start(f32[3,8,4,256]{3,2,1,0:T(4,128)} %start_ref.5) | copy-start | bytes 294916
  21.3 15.6 %copy-start.6 = (f32[3,8,4,256]{3,2,1,0:T(4,128)S(1)}, f32[3,8,4,256]{3,2,1,0:T(4,128)}, u32[]{:S(2)}) copy-start(f32[3,8,4,256]{3,2,1,0:T(4,128)} %load_ref.1) | copy-start | bytes 294916
  21.3 15.6 %copy-start.8 = (f32[8,4,256]{2,1,0:T(4,128)S(1)}, f32[8,4,256]{2,1,0:T(4,128)}, u32[]{:S(2)}) copy-start(f32[8,4,256]{2,1,0:T(4,128)} %stiff_in_ref.1) | copy-start | bytes 98308
  29.8 7.9 %collective-permute-start.3 = (f32[256,512]{1,0:T(8,128)S(1)}, f32[256,512]{1,0:T(8,128)S(1)}, u32[]{:S(2)}, u32[]{:S(2)}) collective-permute-start(f32[256,512]{1,0:T(8,128)S(1)} %get-tuple-element.93), channel_id=1, source_target_pairs={{1,2},{3,4},{5,6},{7,8},{9,10},{11,12},{13,14},{15,16},{17,18},{19... | collective-permute-start | bytes 1572872 | tf_op jit(solution)/shard_map/ppermute | solution.py:71
  30.5 7.9 %collective-permute-start.2 = (f32[256,512]{1,0:T(8,128)S(1)}, f32[256,512]{1,0:T(8,128)S(1)}, u32[]{:S(2)}, u32[]{:S(2)}) collective-permute-start(f32[256,512]{1,0:T(8,128)S(1)} %get-tuple-element.92), channel_id=1, source_target_pairs={{0,1},{1,0},{2,3},{3,2},{4,5},{5,4},{6,7},{7,6},{8,9},{9,8},{10,11... | collective-permute-start | bytes 1572872 | tf_op jit(solution)/shard_map/ppermute | solution.py:71
  37.0 0.7 collective-permute-start.4
  38.4 14.6 %copy-start.1 = (f32[32,6,1024]{2,0,1:T(8,128)S(1)}, f32[32,6,1024]{2,0,1:T(8,128)}, u32[]{:S(2)}) copy-start(f32[32,6,1024]{2,0,1:T(8,128)} %param.22) | copy-start | bytes 2359300
  40.7 39.0 %collective-permute-start.7 = (f32[256,512]{1,0:T(8,128)S(1)}, f32[256,512]{1,0:T(8,128)S(1)}, u32[]{:S(2)}, u32[]{:S(2)}) collective-permute-start(f32[256,512]{1,0:T(8,128)S(1)} %get-tuple-element.105), channel_id=1, source_target_pairs={{1,2},{3,4},{5,6},{7,8},{9,10},{11,12},{13,14},{15,16},{17,18},{19... | collective-permute-start | bytes 1572872 | tf_op jit(solution)/shard_map/ppermute | solution.py:71
  41.4 38.3 %collective-permute-start.5 = (f32[256,512]{1,0:T(8,128)S(1)}, f32[256,512]{1,0:T(8,128)S(1)}, u32[]{:S(2)}, u32[]{:S(2)}) collective-permute-start(f32[256,512]{1,0:T(8,128)S(1)} %get-tuple-element.103), channel_id=1, source_target_pairs={{0,1},{1,0},{2,3},{3,2},{4,5},{5,4},{6,7},{7,6},{8,9},{9,8},{10,11... | collective-permute-start | bytes 1572872 | tf_op jit(solution)/shard_map/ppermute | solution.py:71
  51.3 1.7 collective-permute-start.6
  82.0 20.2 %collective-permute-start.9 = (f32[256,512]{1,0:T(8,128)S(1)}, f32[256,512]{1,0:T(8,128)S(1)}, u32[]{:S(2)}, u32[]{:S(2)}) collective-permute-start(f32[256,512]{1,0:T(8,128)S(1)} %get-tuple-element.113), channel_id=1, source_target_pairs={{1,2},{3,4},{5,6},{7,8},{9,10},{11,12},{13,14},{15,16},{17,18},{19... | collective-permute-start | bytes 1572872 | tf_op jit(solution)/shard_map/ppermute | solution.py:71
  82.7 19.5 %collective-permute-start.8 = (f32[256,512]{1,0:T(8,128)S(1)}, f32[256,512]{1,0:T(8,128)S(1)}, u32[]{:S(2)}, u32[]{:S(2)}) collective-permute-start(f32[256,512]{1,0:T(8,128)S(1)} %get-tuple-element.111), channel_id=1, source_target_pairs={{0,1},{1,0},{2,3},{3,2},{4,5},{5,4},{6,7},{7,6},{8,9},{9,8},{10,11... | collective-permute-start | bytes 1572872 | tf_op jit(solution)/shard_map/ppermute | solution.py:71
  104.5 30.4 %copy-start.3 = (f32[32,6,1024]{2,0,1:T(8,128)S(1)}, f32[32,6,1024]{2,0,1:T(8,128)}, u32[]{:S(2)}) copy-start(f32[32,6,1024]{2,0,1:T(8,128)} %param.23) | copy-start | bytes 2359300
  104.5 40.3 %collective-permute-start.10 = (f32[256,512]{1,0:T(8,128)S(1)}, f32[256,512]{1,0:T(8,128)S(1)}, u32[]{:S(2)}, u32[]{:S(2)}) collective-permute-start(f32[256,512]{1,0:T(8,128)S(1)} %get-tuple-element.121), channel_id=1, source_target_pairs={{0,1},{1,0},{2,3},{3,2},{4,5},{5,4},{6,7},{7,6},{8,9},{9,8},{10,11... | collective-permute-start | bytes 1572872 | tf_op jit(solution)/shard_map/ppermute | solution.py:71
  104.6 40.2 %collective-permute-start.11 = (f32[256,512]{1,0:T(8,128)S(1)}, f32[256,512]{1,0:T(8,128)S(1)}, u32[]{:S(2)}, u32[]{:S(2)}) collective-permute-start(f32[256,512]{1,0:T(8,128)S(1)} %get-tuple-element.122), channel_id=1, source_target_pairs={{1,2},{3,4},{5,6},{7,8},{9,10},{11,12},{13,14},{15,16},{17,18},{19... | collective-permute-start | bytes 1572872 | tf_op jit(solution)/shard_map/ppermute | solution.py:71
  153.2 3.2 %collective-permute-start.13 = (f32[256,512]{1,0:T(8,128)S(1)}, f32[256,512]{1,0:T(8,128)S(1)}, u32[]{:S(2)}, u32[]{:S(2)}) collective-permute-start(f32[256,512]{1,0:T(8,128)S(1)} %get-tuple-element.136), channel_id=1, source_target_pairs={{1,2},{3,4},{5,6},{7,8},{9,10},{11,12},{13,14},{15,16},{17,18},{19... | collective-permute-start | bytes 1572872 | tf_op jit(solution)/shard_map/ppermute | solution.py:71
  153.9 3.3 %collective-permute-start.12 = (f32[256,512]{1,0:T(8,128)S(1)}, f32[256,512]{1,0:T(8,128)S(1)}, u32[]{:S(2)}, u32[]{:S(2)}) collective-permute-start(f32[256,512]{1,0:T(8,128)S(1)} %get-tuple-element.135), channel_id=1, source_target_pairs={{0,1},{1,0},{2,3},{3,2},{4,5},{5,4},{6,7},{7,6},{8,9},{9,8},{10,11... | collective-permute-start | bytes 1572872 | tf_op jit(solution)/shard_map/ppermute | solution.py:71
  155.7 0.7 collective-permute-start.14
  159.5 29.3 %collective-permute-start.17 = (f32[256,512]{1,0:T(8,128)S(1)}, f32[256,512]{1,0:T(8,128)S(1)}, u32[]{:S(2)}, u32[]{:S(2)}) collective-permute-start(f32[256,512]{1,0:T(8,128)S(1)} %get-tuple-element.145), channel_id=1, source_target_pairs={{1,2},{3,4},{5,6},{7,8},{9,10},{11,12},{13,14},{15,16},{17,18},{19... | collective-permute-start | bytes 1572872 | tf_op jit(solution)/shard_map/ppermute | solution.py:71
  160.2 28.6 %collective-permute-start.15 = (f32[256,512]{1,0:T(8,128)S(1)}, f32[256,512]{1,0:T(8,128)S(1)}, u32[]{:S(2)}, u32[]{:S(2)}) collective-permute-start(f32[256,512]{1,0:T(8,128)S(1)} %get-tuple-element.143), channel_id=1, source_target_pairs={{0,1},{1,0},{2,3},{3,2},{4,5},{5,4},{6,7},{7,6},{8,9},{9,8},{10,11... | collective-permute-start | bytes 1572872 | tf_op jit(solution)/shard_map/ppermute | solution.py:71
  173.7 1.5 collective-permute-start.16
  191.1 2.0 collective-permute-start.18
  191.2 1.9 collective-permute-start.19
where the time goes:
time: 241 us
  blocking collectives  117 us (49%)
  Pallas kernels  57.5 us (24%)
  starting transfers between devices  48.5 us (20%)
  waiting for transfers between devices  11.6 us (5%)
  other arithmetic  2.77 us (1%)
    all_to_all x8, blocking collectives, exchange(): return lax.all_to_all(send, AXES, split_axis=0, concat_axis=0, tiled=True)  117 us
    ppermute x20, starting transfers between devices, swap(): return (lax.ppermute(near, AXES, first), lax.ppermute(far, AXES, second))  41.2 us
    pallas_call x8, Pallas kernels, local(): call(functools.partial(sweep_kernel, rows, most, spot, opening, closing,...  35.5 us
    all_to_all x1, starting transfers between devices, exchange(): return lax.all_to_all(send, AXES, split_axis=0, concat_axis=0, tiled=True)  7.32 us
    all_to_all x1, waiting for transfers between devices, exchange(): return lax.all_to_all(send, AXES, split_axis=0, concat_axis=0, tiled=True)  6.09 us
    ppermute x20, waiting for transfers between devices, swap(): return (lax.ppermute(near, AXES, first), lax.ppermute(far, AXES, second))  5.47 us
    pallas_call x1, Pallas kernels, local(): call(functools.partial(gather_kernel, most), [((devices, LANES * -(-most...  5.18 us
  transfers between devices with their start and end apart: 21, of which 6 were waited for; matrix products, arithmetic and copies ran while one was open for 0% of the time, Pallas kernels for 6%

commit v1 on v0

--- a/solution.py
+++ b/solution.py
@@ -68,7 +68,8 @@
 
 def swap(near, far):
     first, second = pairs()
-    return lax.ppermute(near, AXES, first), lax.ppermute(far, AXES, second)
+    far = lax.ppermute(far, AXES, second)
+    return lax.ppermute(near, AXES, first), far
 
 
 def onehots(owner, rank, devices, most):
@@ -102,22 +103,23 @@
     send_ref[:, most : 2 * most] = dot(named, placed * flux, ((1,), (1,)))
 
 
-def tiled_place(cell, depth):
-    across = depth // LANES
+def places(cell, rows, depth):
     row, along = cell // depth, cell % depth
-    tile = (row // SUB) * across + along // LANES
-    return (tile * SUB + row % SUB) * LANES + along % LANES
+    line = (along // LANES) * rows + row
+    lane = along % LANES
+    inside = (line % SUB) * LANES + lane
+    return (line - line % SUB) * (SUB * LANES) + inside, line * LANES + lane
 
 
 def scatter_cells(most, first, code_ref, value_ref, grids):
     count = len(grids)
     place = iota((SUB, LANES), 0) * LANES + iota((SUB, LANES), 1)
     area = SUB * LANES
-    fill = 8
+    fill = 64
 
     def clear(step, carry):
         for grid in grids:
-            grid[pl.ds(step * fill, fill)] = jnp.zeros((fill, SUB, LANES), F32)
+            grid[pl.ds(pl.multiple_of(step * fill, fill), fill), :] = jnp.zeros((fill, LANES), F32)
         return carry
 
     lax.fori_loop(0, grids[0].shape[0] // fill, clear, 0)
@@ -126,7 +128,8 @@
     def outer(d, carry):
         for slot in range(most):
             codes = [code_ref[g * part + d, slot] for g in range(count)]
-            tiles = [lax.shift_right_logical(code, area.bit_length() - 1) for code in codes]
+            tiles = [pl.multiple_of(lax.shift_right_logical(code, area.bit_length() - 1), SUB) for code in codes]
+            tiles = [(pl.ds(tile, SUB), slice(None)) for tile in tiles]
             added = [
                 grid[tile] + jnp.where(place == (code & (area - 1)), value_ref[g * part + d, first + slot], 0.0)
                 for g, (grid, tile, code) in enumerate(zip(grids, tiles, codes))
@@ -165,22 +168,11 @@
         out_ref[d : d + 1, 0:most] = found[0:1, d * most : (d + 1) * most]
 
 
-def gather_kernel(most, code_ref, field_ref, out_ref, lines_ref, flat_ref):
-    across = field_ref.shape[1] // LANES
-
-    def flatten(j, carry):
-        for k in range(2):
-            for t in range(across):
-                to = pl.ds(pl.multiple_of(((2 * j + k) * across + t) * SUB, SUB), SUB)
-                at = pl.ds(pl.multiple_of((2 * j + k) * SUB, SUB), SUB)
-                flat_ref[to, :] = field_ref[at, t * LANES : (t + 1) * LANES]
-        return carry
-
-    lax.fori_loop(0, field_ref.shape[0] // (2 * SUB), flatten, 0)
-    gather_cells(most, code_ref, flat_ref, None, out_ref, lines_ref)
-
-
-def sweep_kernel(rows, most, first, opening, closing, sending, carrying, *refs):
+def gather_kernel(most, code_ref, field_ref, extra_ref, out_ref, lines_ref):
+    gather_cells(most, code_ref, field_ref, extra_ref, out_ref, lines_ref)
+
+
+def sweep_kernel(rows, most, first, opening, closing, sending, carrying, fetching, *refs):
     refs = list(refs)
     me_ref, field_ref, near_ref, far_ref, rhs_ref, scale_ref = refs[:6]
     del refs[:6]
@@ -194,67 +186,97 @@
     grids = []
     if opening:
         source_ref, *grids = refs
+        copies = []
+        scaled_ref = grids.pop(0) if fetching else None
+        if fetching:
+            *grids, field_in, rhs_in, scale_in, sems = grids
+            moves = ((field_ref, field_in), (rhs_ref, rhs_in), (scale_ref, scale_in))
+            copies = [pltpu.make_async_copy(source, into, sems.at[i]) for i, (source, into) in enumerate(moves)]
+            field_ref, rhs_ref, scale_ref = field_in, rhs_in, scale_in
+        for copy in copies:
+            copy.start()
         scatter_cells(most, first, code_ref, value_ref, grids)
+        for copy in copies:
+            copy.wait()
     if closing:
         sampled_ref, lines_ref, flat_ref = refs
     wide, depth = near_ref.shape
     across = depth // LANES
-    sub = iota((SUB, depth), 0)
-    lane = iota((SUB, depth), 1)
+    sub = iota((SUB, LANES), 0)
+    lane = iota((SUB, LANES), 1)
     even = (me_ref[0] & 1) == 0
     blocks = wide // SUB
     unroll = 2
 
-    def block(j):
+    zero = jnp.zeros((SUB, LANES), F32)
+    total = rows * wide
+    strips = field_ref.shape[1] == LANES
+
+    def block(j, first_block=False, last_block=False):
         y = pl.multiple_of(j * SUB, SUB)
-        above = pl.multiple_of(jnp.maximum(j - 1, 0) * SUB, SUB)
-        below = pl.multiple_of(jnp.minimum(j + 1, blocks - 1) * SUB, SUB)
-        top = (sub == 0) & (j == 0)
-        bottom = (sub == SUB - 1) & (j == blocks - 1)
-        near, far = near_ref[pl.ds(y, SUB), :], far_ref[pl.ds(y, SUB), :]
-        low, high = jnp.where(even, far, near), jnp.where(even, near, far)
-        tiles = [field_ref[pl.ds(x * wide + y, SUB), :] for x in range(rows)]
-        edge = []
-        for x, here in enumerate(tiles):
-            spot = pl.ds(x * wide + y, SUB)
-            over = field_ref[pl.ds(x * wide + above, SUB), :]
-            under = field_ref[pl.ds(x * wide + below, SUB), :]
-            beside = (low if x == 0 else tiles[x - 1]) + (high if x == rows - 1 else tiles[x + 1])
-            ahead = pltpu.roll(jnp.where(sub == SUB - 1, over, here), 1, 0)
-            behind = pltpu.roll(jnp.where(sub == 0, under, here), SUB - 1, 0)
-            beside = beside + jnp.where(top, 0.0, ahead)
-            beside = beside + jnp.where(bottom, 0.0, behind)
-            beside = beside + jnp.where(lane == 0, 0.0, pltpu.roll(here, 1, 1))
-            beside = beside + jnp.where(lane == depth - 1, 0.0, pltpu.roll(here, depth - 1, 1))
-            rhs = rhs_ref[spot, :]
-            at = (x * blocks + j) * across
-            if grids:
-                parts = []
-                for t in range(across):
-                    part = grids[0][at + t]
-                    for grid in grids[1:]:
-                        part = part + grid[at + t]
-                    parts.append(part)
-                rhs = rhs + jnp.concatenate(parts, axis=1)
-                source_ref[spot, :] = rhs
-            new = (1.0 - OMEGA) * here + (rhs + beside) * scale_ref[spot, :]
-            out_ref[spot, :] = new
-            if closing:
-                for t in range(across):
-                    to = pl.ds(pl.multiple_of((at + t) * SUB, SUB), SUB)
-                    flat_ref[to, :] = new[:, t * LANES : (t + 1) * LANES]
-            if x in (0, rows - 1):
-                edge.append(new)
-        if sending:
-            sends[0][pl.ds(y, SUB), :] = jnp.where(even, edge[1], edge[0])
-            sends[1][pl.ds(y, SUB), :] = jnp.where(even, edge[0], edge[1])
+
+        def tile(start, t):
+            if strips:
+                return field_ref[pl.ds(start + t * total, SUB), :]
+            return field_ref[pl.ds(start, SUB), t * LANES : (t + 1) * LANES]
+
+        for t in range(across):
+            strip = slice(t * LANES, (t + 1) * LANES)
+            near, far = near_ref[pl.ds(y, SUB), strip], far_ref[pl.ds(y, SUB), strip]
+            low, high = jnp.where(even, far, near), jnp.where(even, near, far)
+            edge = []
+            for x in range(rows):
+                start = pl.multiple_of(x * wide + y, SUB)
+                spot = pl.ds(start, SUB)
+                here = tile(start, t)
+                beside = low if x == 0 else tile(start - wide, t)
+                beside = beside + (high if x == rows - 1 else tile(start + wide, t))
+                if strips and not first_block:
+                    beside = beside + tile(start - 1, t)
+                else:
+                    over = zero if first_block else tile(start - SUB, t)
+                    beside = beside + pltpu.roll(jnp.where(sub == SUB - 1, over, here), 1, 0)
+                if strips and not last_block:
+                    beside = beside + tile(start + 1, t)
+                else:
+                    under = zero if last_block else tile(start + SUB, t)
+                    beside = beside + pltpu.roll(jnp.where(sub == 0, under, here), SUB - 1, 0)
+                left = tile(start, t - 1) if t > 0 else zero
+                right = tile(start, t + 1) if t < across - 1 else zero
+                beside = beside + pltpu.roll(jnp.where(lane == LANES - 1, left, here), 1, 1)
+                beside = beside + pltpu.roll(jnp.where(lane == 0, right, here), LANES - 1, 1)
+                rhs = rhs_ref[spot, strip]
+                lines = pl.ds(pl.multiple_of(start + t * total, SUB), SUB)
+                if grids:
+                    for grid in grids:
+                        rhs = rhs + grid[lines, :]
+                    source_ref[spot, strip] = rhs
+                scale = scale_ref[spot, strip]
+                if fetching:
+                    scale = OMEGA / (6.0 + scale)
+                    scaled_ref[spot, strip] = scale
+                new = (1.0 - OMEGA) * here + (rhs + beside) * scale
+                if closing:
+                    out_ref[spot, strip] = new
+                    flat_ref[lines, :] = new
+                else:
+                    out_ref[lines, :] = new
+                if x in (0, rows - 1):
+                    edge.append(new)
+            if sending:
+                sends[0][pl.ds(y, SUB), strip] = jnp.where(even, edge[1], edge[0])
+                sends[1][pl.ds(y, SUB), strip] = jnp.where(even, edge[0], edge[1])
 
     def step(j, carry):
         for k in range(unroll):
-            block(j * unroll + k)
+            block(1 + j * unroll + k)
         return carry
 
-    lax.fori_loop(0, blocks // unroll, step, 0)
+    block(0, first_block=True)
+    lax.fori_loop(0, (blocks - 2) // unroll, step, 0)
+    for j in range(1 + (blocks - 2) // unroll * unroll, blocks - 1):
+        block(j)
+    block(blocks - 1, last_block=True)
     if closing:
         gather_cells(most, code_ref, flat_ref, extra_ref, sampled_ref, lines_ref)
 
@@ -335,7 +357,7 @@
             at += deep
 
 
-def wall_first_kernel(devices, layers, me_ref, start_ref, load_ref, stiff_in_ref, state_ref, near_ref, far_ref, past_ref,
+def wall_first_kernel(devices, layers, me_ref, start_ref, load_ref, stiff_in_ref, state_ref, near_ref, far_ref, gram_ref,
                       send_ref, base_ref, stiff_ref, force_ref, image_ref, twice_ref, wide_ref):
     rows, turns = start_ref.shape[2:]
     lead = (SUB - rows) // 2
@@ -373,12 +395,18 @@
     for c in range(3):
         force[c * layers] = force[c * layers] + wide_ref[2 * tiles + layers + c]
     square, product = wall_parts(force, stiff, layers, valid, own, force_ref, image_ref, twice_ref)
+    lanes = iota((1, LANES), 1)
+    row = jnp.where(lanes < 2, two_lanes(square, product, LANES), summed(gram_ref))
+    send_ref[...] = jnp.broadcast_to(row, send_ref.shape)
+
+
+def gram_kernel(devices, past_ref, send_ref):
     history = past_ref.shape[1]
     gram = jnp.zeros((history, history), F32)
     for c in range(past_ref.shape[0]):
         gram = gram + dot(past_ref[c], past_ref[c], ((1,), (1,)))
-    send_ref[...] = jnp.broadcast_to(two_lanes(square, product, LANES), (devices, LANES))
     chunk = history * history // devices
+    send_ref[...] = jnp.zeros_like(send_ref)
     for d in range(devices):
         row, left = d * chunk // history, d * chunk % history
         send_ref[d : d + 1, 2 : 2 + chunk] = gram[row : row + 1, left : left + chunk]
@@ -432,28 +460,32 @@
     send_ref[...] = jnp.broadcast_to(row, send_ref.shape)
 
 
-def wall_last_kernel(layers, rows, at, one_ref, two_ref, force_ref, image_ref, start_ref, wall_ref, solid_ref):
+def wall_steps(at, one_ref, two_ref):
     one = summed(one_ref)
     two = jnp.sum(two_ref[:, at : at + 2], axis=0, keepdims=True)
     norm, alpha = one[:, 0:1], one[:, 0:1] / one[:, 1:2]
     newer = two[:, 0:1]
     ratio = newer / norm
-    beta = newer / (two[:, 1:2] - ratio * newer / alpha)
-    turns = force_ref.shape[2]
+    return alpha, newer / (two[:, 1:2] - ratio * newer / alpha), ratio
+
+
+def moved_tile(index, steps, layers, rows, force_ref, image_ref, start_ref):
+    alpha, beta, ratio = steps
     lead = (SUB - rows) // 2
+    force = force_ref[index]
+    residual = force - alpha * image_ref[index]
+    moved = alpha * force + beta * (residual + ratio * force)
+    return start_ref[index // layers, index % layers] + moved[lead : lead + rows, :]
+
+
+def wall_last_kernel(layers, rows, at, one_ref, two_ref, force_ref, image_ref, start_ref, wall_ref):
+    steps = wall_steps(at, one_ref, two_ref)
     for i in range(force_ref.shape[0]):
-        c, layer = i // layers, i % layers
-        force = force_ref[i]
-        residual = force - alpha * image_ref[i]
-        moved = alpha * force + beta * (residual + ratio * force)
-        wall = start_ref[c, layer] + moved[lead : lead + rows, :]
-        wall_ref[c, layer] = wall
-        if layer == 0:
-            for s in range(rows):
-                solid_ref[c : c + 1, s * turns : (s + 1) * turns] = wall[s : s + 1, :]
-
-
-def returned_kernel(devices, most, turn, got_ref, owner_ref, rank_ref, normals_ref, state_ref, solid_ref, past_ref, *rest):
+        wall_ref[i // layers, i % layers] = moved_tile(i, steps, layers, rows, force_ref, image_ref, start_ref)
+
+
+def returned_kernel(devices, most, turn, layers, rows, got_ref, owner_ref, rank_ref, normals_ref, state_ref, past_ref,
+                    one_ref, force_ref, image_ref, start_ref, *rest):
     if turn == 0:
         output_ref, resid_ref, send_ref = rest
     else:
@@ -461,7 +493,12 @@
     named, placed = onehots(owner_ref[...], rank_ref[...], devices, most)
     spread = dot(got_ref[:, 0:most], named, ((0,), (0,)))
     sampled = jnp.sum(spread * placed, axis=0, keepdims=True)
-    output_ref[0:3, :] = solid_ref[...]
+    steps = wall_steps(most, one_ref, got_ref)
+    turns = start_ref.shape[3]
+    for c in range(3):
+        tile = moved_tile(c * layers, steps, layers, rows, force_ref, image_ref, start_ref)
+        for s in range(rows):
+            output_ref[c : c + 1, s * turns : (s + 1) * turns] = tile[s : s + 1, :]
     output_ref[3:6, :] = -sampled * normals_ref[...]
     resid_ref[...] = output_ref[...] - state_ref[...]
     history = past_ref.shape[1]
@@ -613,13 +650,15 @@
         [vmem()] * 4, limit=4,
     )(owner, fluid_cell.reshape(1, points), normals, interface_start)
     got = exchange(send)
-    got, coef, start_in, load_in, state = tie(got, fluid_coef, wall_start, wall_load, interface_start)
-    cells = tiled_place(jnp.maximum(got[:, 0:most].astype(jnp.int32) - 1, 0), depth)
+    got, start_in, load_in, state = tie(got, wall_start, wall_load, interface_start)
+    into, cells = places(jnp.maximum(got[:, 0:most].astype(jnp.int32) - 1, 0), flat[0], depth)
+    thin = (flat[0] * depth // LANES, LANES)
     flux, spot = got, most
-    scale = (OMEGA / (6.0 + coef)).reshape(flat)
+    scale = fluid_coef.reshape(flat)
 
     needed = (3 * (lead + 1) + 3 * lead + lead) * layers + 3 * lead
     packed = (SUB * -(-needed // SUB), turns)
+    gram = call(functools.partial(gram_kernel, devices), [((devices, LANES), F32)], [vmem()], limit=4)(past_r)[0]
     packs = call(
         functools.partial(pack_kernel, layers, wall_rows),
         [(packed, F32)] * 2, [smem()] + [vmem()] * 4, [pltpu.VMEM((3, wall_rows, turns), F32)], limit=2,
@@ -627,18 +666,21 @@
 
     small = ((devices, LANES), F32)
     padded = LANES * -(-2 * history // LANES)
-    output = resid = wall = None
+    output = resid = None
     for turn in range(COUPLE):
         for sweep in range(SWEEPS):
             last = sweep + 1 == SWEEPS
             sending = not last or turn + 1 < COUPLE
             opening, closing = sweep == 0, not sending
-            carrying = turn > 0
+            carrying, fetching = turn > 0, opening and turn == 0
+            big = pl.BlockSpec(memory_space=pl.ANY) if fetching else vmem()
             extra_in, extra_spec, extra_out, scratch = [], [], [], []
             if opening:
-                extra_in, extra_spec = [cells, flux], [smem(), smem()]
-                extra_out = [(flat, F32)]
-                scratch = [pltpu.VMEM((flat[0] * depth // (SUB * LANES), SUB, LANES), F32)] * GRIDS
+                extra_in, extra_spec = [into, flux], [smem(), smem()]
+                extra_out = [(flat, F32)] * (2 if turn == 0 else 1)
+                scratch = [pltpu.VMEM(thin, F32)] * GRIDS
+                if turn == 0:
+                    scratch = scratch + [pltpu.VMEM(flat, F32)] * 3 + [pltpu.SemaphoreType.DMA((3,))]
             if closing:
                 extra_in, extra_spec = [cells], [smem()]
                 if carrying:
@@ -648,33 +690,36 @@
                     )(one, force, image, twice)[0]
                     extra_in, extra_spec = [cells, sums], [smem(), vmem()]
                 extra_out = [((devices, LANES * -(-(most + 2) // LANES)), F32)]
-                scratch = [pltpu.VMEM((devices * most, LANES), F32), pltpu.VMEM((flat[0] * depth // LANES, LANES), F32)]
+                scratch = [pltpu.VMEM((devices * most, LANES), F32), pltpu.VMEM(thin, F32)]
             field, *rest = call(
-                functools.partial(sweep_kernel, rows, most, spot, opening, closing, sending, carrying),
-                [(flat, F32)] + [(plane, F32)] * (2 if sending else 0) + extra_out,
-                [smem()] + [vmem()] * 5 + extra_spec, scratch, limit=26 if opening else 12,
+                functools.partial(sweep_kernel, rows, most, spot, opening, closing, sending, carrying, fetching),
+                [(flat if closing else thin, F32)] + [(plane, F32)] * (2 if sending else 0) + extra_out,
+                [smem(), big, vmem(), vmem(), big, big] + extra_spec, scratch, limit=(44 if fetching else 26) if opening else 12,
             )(me, field, near, far, rhs if opening else source, scale, *extra_in)
             if sending:
                 ends, rest = rest[:2], rest[2:]
             if opening:
                 source = rest[0]
+                scale = rest[-1] if fetching else scale
             if closing:
                 sampled = rest[0]
             elif last:
                 near, far = swap(*ends)
                 sampled = call(
                     functools.partial(gather_kernel, most),
-                    [((devices, LANES * -(-most // LANES)), F32)],
-                    [smem(), vmem()],
-                    [pltpu.VMEM((devices * most, LANES), F32), pltpu.VMEM((flat[0] * depth // LANES, LANES), F32)],
+                    [((devices, LANES * -(-(most + 2) // LANES)), F32)],
+                    [smem(), vmem(), vmem()],
+                    [pltpu.VMEM((devices * most, LANES), F32)],
                     limit=12,
-                )(cells, field)[0]
+                )(cells, field, sums)[0]
             else:
                 near, far = swap(*ends)
             if turn == 0 and sweep == 0:
                 packs, _ = tie(packs, ends)
                 pack_near, pack_far = swap(*packs)
-                far, pack_far = tie(far, pack_far)
+                gram, _ = tie(gram, ends)
+                gram = exchange(gram)
+                far, pack_far, gram = tie(far, pack_far, gram)
             if turn == 0 and sweep == 1:
                 pack_near, ends = tie(pack_near, ends)
                 sums, base, stiff, force, image, twice = call(
@@ -682,26 +727,21 @@
                     [small, (tile, F32), ((layers, SUB, turns), F32)] + [(tile, F32)] * 3,
                     [smem()] + [vmem()] * 7,
                     [pltpu.VMEM((2 * tiles + layers + 3, SUB, turns), F32)], limit=6,
-                )(me, start_in, load_in, wall_stiff, state, pack_near, pack_far, past_r)
+                )(me, start_in, load_in, wall_stiff, state, pack_near, pack_far, gram)
                 one = exchange(sums)
                 one, far = tie(one, far)
             if turn == 0 and sweep == 2:
                 one, ends = tie(one, ends)
                 sums = call(
                     functools.partial(wall_second_kernel, wall_rows),
-                    [small], [vmem()] * 4, limit=2,
+                    [((SUB, LANES), F32)], [vmem()] * 4, limit=2,
                 )(one, force, image, twice)[0]
-                two = exchange(sums)
                 inverse = call(
                     functools.partial(inverse_kernel, history),
                     [((history, history), F32)], [vmem()], [pltpu.VMEM((2 * history, padded), F32)], limit=2,
-                )(two)[0]
-                wall, solid = call(
-                    functools.partial(wall_last_kernel, layers, wall_rows, 0),
-                    [(wall_start.shape, F32), ((3, points), F32)], [vmem()] * 5, limit=2,
-                )(one, two, force, image, wall_start)
-                inverse, far, solid = tie(inverse, far, solid)
-                grams = two
+                )(one)[0]
+                inverse, far, sums = tie(inverse, far, sums)
+                grams = one
             if turn == 1 and sweep == 0:
                 pulls, ends = tie(pulls, ends)
                 pull_near, pull_far = swap(*pulls)
@@ -717,18 +757,13 @@
                 one = exchange(sums)
                 one, far = tie(one, far)
         back = exchange(sampled)
-        if turn + 1 == COUPLE:
-            wall, solid = call(
-                functools.partial(wall_last_kernel, layers, wall_rows, most),
-                [(wall_start.shape, F32), ((3, points), F32)], [vmem()] * 5, limit=2,
-            )(one, back, force, image, wall_start)
         last_args = () if turn == 0 else (resid,)
         before = output
         output, resid, sums = call(
-            functools.partial(returned_kernel, devices, most, turn),
+            functools.partial(returned_kernel, devices, most, turn, layers, wall_rows),
             [((6, points), F32), ((6, points), F32), ((devices, LANES * -(-(2 * history + 2) // LANES)), F32)],
-            [vmem()] * (7 + len(last_args)), limit=4,
-        )(back, owner, rank, normals, state, solid, past_r, *last_args)
+            [vmem()] * (10 + len(last_args)), limit=4,
+        )(back, owner, rank, normals, state, past_r, one, force, image, wall_start, *last_args)
         if turn + 1 < COUPLE:
             sums, inverse = tie(sums, inverse)
         total = exchange(sums)
@@ -741,6 +776,10 @@
             flux, spot = exchange(flux), 0
             flux, pulls = tie(flux, pulls)
         else:
+            wall = call(
+                functools.partial(wall_last_kernel, layers, wall_rows, most),
+                [(wall_start.shape, F32)], [vmem()] * 5, limit=2,
+            )(one, back, force, image, wall_start)[0]
             work = [pltpu.VMEM((SUB * -(-(history + 1) // SUB), padded), F32)]
             state = call(
                 finish_kernel, [((6, points), F32)], [vmem()] * 5, work, limit=4,

time: 241 us -> 233 us (0.967)
  starting transfers between devices: 48.5 us -> 38.8 us
  blocking collectives: 117 us -> 123 us
    all_to_all x8, blocking collectives: 117 us -> 123 us  [exchange(): return lax.all_to_all(send, AXES, split_axis=0, concat_axis=0, tiled=True)]
    ppermute x20, starting transfers between devices: 41.2 us -> 36.3 us  [the longest x10 29.3 us: swap(): return (lax.ppermute(near, AXES, first), far)]
    all_to_all x1, starting transfers between devices: 7.32 us -> 2.46 us  [exchange(): return lax.all_to_all(send, AXES, split_axis=0, concat_axis=0, tiled=True)]
    pallas_call x5 -> x4, Pallas kernels: 9.84 us -> 9.63 us  [the longest x1 4.75 us: local(): call(functools.partial(gather_kernel, most), [((devices, LANES * -(-(most...]
  transfers between devices with their start and end apart: 21 -> 21, of which waited for: 6 -> 5; matrix products, arithmetic and copies ran while one was open for 0% -> 0% of each run, Pallas kernels for 6% -> 6%
where the time goes in v1:
time: 233 us; the launch traced here: 232 us
  blocking collectives  123 us (53%)
  Pallas kernels  57.8 us (25%)
  starting transfers between devices  38.8 us (17%)
  waiting for transfers between devices  10.8 us (5%)
    all_to_all x8, blocking collectives, exchange(): return lax.all_to_all(send, AXES, split_axis=0, concat_axis=0, tiled=True)  123 us
    pallas_call x8, Pallas kernels, local(): call(functools.partial(sweep_kernel, rows, most, spot, opening, closing,...  36.8 us
    ppermute x10, starting transfers between devices, swap(): return (lax.ppermute(near, AXES, first), far)  29.3 us
    ppermute x10, starting transfers between devices, swap(): far = lax.ppermute(far, AXES, second)  7.03 us
    all_to_all x1, waiting for transfers between devices, exchange(): return lax.all_to_all(send, AXES, split_axis=0, concat_axis=0, tiled=True)  6.08 us
    pallas_call x1, Pallas kernels, local(): call(functools.partial(gather_kernel, most), [((devices, LANES * -(-(most...  4.75 us
    ppermute x10, waiting for transfers between devices, swap(): return (lax.ppermute(near, AXES, first), far)  4.71 us
  transfers between devices with their start and end apart: 21, of which 5 were waited for; matrix products, arithmetic and copies ran while one was open for 0% of the time, Pallas kernels for 6%

profile of v1, /device:TPU:0, one launch (start us, length us, event | category | flops | bytes accessed | tf_op | source)
XLA Modules:
  0.0 232.4 jit_solution(12638443603082910776)
XLA Ops:
  0.7 1.3 select_bitcast_fusion
  2.0 0.6 collective-permute-start
  2.6 0.7 collective-permute-start.1
  3.3 0.8 shard_map.139
  4.1 19.4 %all_to_all.104 = f32[32,1,128]{2,1,0:T(1,128)S(1)} all-to-all(f32[32,1,128]{2,1,0:T(1,128)S(1)} %bitcast.83), channel_id=1, replica_groups=mesh['solver'=4,'space'=8] {'solver','space'}, dimensions={0} | all-to-all | bytes 32768 | tf_op jit(solution)/shard_map/all_to_all | solution.py:55
  23.5 0.1 multiply_add_fusion
  23.5 0.0 copy-start.3
  23.5 0.0 copy-start.5
  23.6 0.0 copy-start.7
  23.6 0.0 copy-start.1
  23.6 8.5 %shard_map.140 = (f32[4096,128]{1,0:T(8,128)S(1)}, f32[256,512]{1,0:T(8,128)S(1)}, f32[256,512]{1,0:T(8,128)S(1)}, f32[1024,512]{1,0:T(8,128)S(1)}, f32[1024,512]{1,0:T(8,128)S(1)}) custom-call(s32[1]{0:T(128)} %bitcast.refs_0_.me_ref, f32[1024,512]{1,0:T(8,128)} %bitcast.85, f32[256,512]{1,0:T(8,128)S(1)} %collective-permute-done.refs_2_, ...), custom_call_target="tpu_custom_call" | custom-call | tf_op jit(solution)/shard_map/pallas_call | solution.py:694
  32.1 0.7 collective-permute-start.3
  32.8 1.7 collective-permute-start.2
  34.5 0.1 shard_map.141
  34.6 0.7 collective-permute-start.4
  35.3 0.8 shard_map.142
  36.1 16.5 %all_to_all.105 = f32[32,1,128]{2,1,0:T(1,128)S(1)} all-to-all(f32[32,1,128]{2,1,0:T(1,128)S(1)} %bitcast.76), channel_id=1, replica_groups=mesh['solver'=4,'space'=8] {'solver','space'}, dimensions={0} | all-to-all | bytes 32768 | tf_op jit(solution)/shard_map/all_to_all | solution.py:55
  52.7 2.4 %shard_map.143 = (f32[4096,128]{1,0:T(8,128)S(1)}, f32[256,512]{1,0:T(8,128)S(1)}, f32[256,512]{1,0:T(8,128)S(1)}) custom-call(s32[1]{0:T(128)} %bitcast.refs_0_.me_ref, f32[4096,128]{1,0:T(8,128)S(1)} %get-tuple-element.89.refs_1_, f32[256,512]{1,0:T(8,128)S(1)} %collective-permute-done.2.refs_2_, f32[256,512]{1,0:T(8,128)S(1)} %collective-permute-done.3.refs_3_, ...), custom_call_target="tpu_custom_call" | custom-call | tf_op jit(solution)/shard_map/pallas_call | solution.py:694
  55.1 0.7 collective-permute-start.7
  55.8 1.9 collective-permute-start.5
  57.7 0.1 collective-permute-start.6
  57.8 1.7 collective-permute-done.6.near_ref
  59.5 0.6 shard_map.144
  60.0 12.9 %all_to_all.106 = f32[32,1,128]{2,1,0:T(1,128)S(1)} all-to-all(f32[32,1,128]{2,1,0:T(1,128)S(1)} %bitcast.79), channel_id=1, replica_groups=mesh['solver'=4,'space'=8] {'solver','space'}, dimensions={0} | all-to-all | bytes 32768 | tf_op jit(solution)/shard_map/all_to_all | solution.py:55
  73.0 2.4 %shard_map.145 = (f32[4096,128]{1,0:T(8,128)S(1)}, f32[256,512]{1,0:T(8,128)S(1)}, f32[256,512]{1,0:T(8,128)S(1)}) custom-call(s32[1]{0:T(128)} %bitcast.refs_0_.me_ref, f32[4096,128]{1,0:T(8,128)S(1)} %get-tuple-element.102.refs_1_, f32[256,512]{1,0:T(8,128)S(1)} %collective-permute-done.5.refs_2_, f32[256,512]{1,0:T(8,128)S(1)} %collective-permute-done.7.refs_3_, ...), custom_call_target="tpu_custom_call" | custom-call | tf_op jit(solution)/shard_map/pallas_call | solution.py:694
  75.4 0.7 collective-permute-start.9
  76.1 1.9 collective-permute-start.8
  78.0 2.8 %shard_map.146.inverse_ref = f32[32,32]{1,0:T(8,128)S(1)} custom-call(f32[32,128]{1,0:T(8,128)S(1)} %bitcast.56), custom_call_target="tpu_custom_call" | custom-call | tf_op jit(solution)/shard_map/pallas_call | solution.py:739
  80.8 0.3 shard_map.147.extra_ref
  81.2 2.4 %shard_map.148 = (f32[4096,128]{1,0:T(8,128)S(1)}, f32[256,512]{1,0:T(8,128)S(1)}, f32[256,512]{1,0:T(8,128)S(1)}) custom-call(s32[1]{0:T(128)} %bitcast.refs_0_.me_ref, f32[4096,128]{1,0:T(8,128)S(1)} %get-tuple-element.111.refs_1_, f32[256,512]{1,0:T(8,128)S(1)} %collective-permute-done.8.refs_2_, f32[256,512]{1,0:T(8,128)S(1)} %collective-permute-done.9.refs_3_, ...), custom_call_target="tpu_custom_call" | custom-call | tf_op jit(solution)/shard_map/pallas_call | solution.py:694
  83.6 0.0 copy-start.2
  83.6 7.6 %collective-permute-start.10 = (f32[256,512]{1,0:T(8,128)S(1)}, f32[256,512]{1,0:T(8,128)S(1)}, u32[]{:S(2)}, u32[]{:S(2)}) collective-permute-start(f32[256,512]{1,0:T(8,128)S(1)} %get-tuple-element.121), channel_id=1, source_target_pairs={{0,1},{1,0},{2,3},{3,2},{4,5},{5,4},{6,7},{7,6},{8,9},{9,8},{10,11... | collective-permute-start | bytes 1572872 | tf_op jit(solution)/shard_map/ppermute | solution.py:72
  91.3 0.7 collective-permute-start.11
  92.0 0.0 copy-start
  92.0 4.7 %shard_map.149 = f32[32,128]{1,0:T(8,128)S(1)} custom-call(s32[32,64]{1,0:T(8,128)S(1)} %get-tuple-element.167.code_ref.refs_6_, f32[4096,128]{1,0:T(8,128)S(1)} %get-tuple-element.120.field_ref.refs_1_, f32[8,128]{1,0:T(8,128)S(1)} %shard_map.147.extra_ref), custom_call_target="tpu_custom_call" | custom-call | tf_op jit(solution)/shard_map/pallas_call | solution.py:708
  96.7 18.0 %all_to_all.107 = f32[32,1,128]{2,1,0:T(1,128)S(1)} all-to-all(f32[32,1,128]{2,1,0:T(1,128)S(1)} %bitcast.74), channel_id=1, replica_groups=mesh['solver'=4,'space'=8] {'solver','space'}, dimensions={0} | all-to-all | bytes 32768 | tf_op jit(solution)/shard_map/all_to_all | solution.py:55
  114.7 1.5 shard_map.150
  116.2 8.9 %all_to_all.108 = f32[32,1,128]{2,1,0:T(1,128)S(1)} all-to-all(f32[32,1,128]{2,1,0:T(1,128)S(1)} %bitcast.81), channel_id=1, replica_groups=mesh['solver'=4,'space'=8] {'solver','space'}, dimensions={0} | all-to-all | bytes 32768 | tf_op jit(solution)/shard_map/all_to_all | solution.py:55
  125.1 1.1 shard_map.151
  126.2 8.9 %all_to_all.109 = f32[32,1,128]{2,1,0:T(1,128)S(1)} all-to-all(f32[32,1,128]{2,1,0:T(1,128)S(1)} %bitcast.82), channel_id=1, replica_groups=mesh['solver'=4,'space'=8] {'solver','space'}, dimensions={0} | all-to-all | bytes 32768 | tf_op jit(solution)/shard_map/all_to_all | solution.py:55
  135.0 8.8 %shard_map.152 = (f32[4096,128]{1,0:T(8,128)S(1)}, f32[256,512]{1,0:T(8,128)S(1)}, f32[256,512]{1,0:T(8,128)S(1)}, f32[1024,512]{1,0:T(8,128)S(1)}) custom-call(s32[1]{0:T(128)} %bitcast.refs_0_.me_ref, f32[4096,128]{1,0:T(8,128)S(1)} %get-tuple-element.120.field_ref.refs_1_, f32[256,512]{1,0:T(8,128)S(1)} %collective-permute-done.10.refs_2_, ...), custom_call_target="tpu_custom_call" | custom-call | tf_op jit(solution)/shard_map/pallas_call | solution.py:694
  143.8 0.7 collective-permute-start.13
  144.5 1.3 collective-permute-start.12
  145.9 0.6 collective-permute-start.14
  146.5 0.9 collective-permute-done.12.refs_2_
  147.4 2.4 %shard_map.153 = (f32[4096,128]{1,0:T(8,128)S(1)}, f32[256,512]{1,0:T(8,128)S(1)}, f32[256,512]{1,0:T(8,128)S(1)}) custom-call(s32[1]{0:T(128)} %bitcast.refs_0_.me_ref, f32[4096,128]{1,0:T(8,128)S(1)} %get-tuple-element.134.refs_1_, f32[256,512]{1,0:T(8,128)S(1)} %collective-permute-done.12.refs_2_, f32[256,512]{1,0:T(8,128)S(1)} %collective-permute-done.13.refs_3_, ...), custom_call_target="tpu_custom_call" | custom-call | tf_op jit(solution)/shard_map/pallas_call | solution.py:694
  149.8 0.7 collective-permute-start.17
  150.5 14.0 %collective-permute-start.15 = (f32[256,512]{1,0:T(8,128)S(1)}, f32[256,512]{1,0:T(8,128)S(1)}, u32[]{:S(2)}, u32[]{:S(2)}) collective-permute-start(f32[256,512]{1,0:T(8,128)S(1)} %get-tuple-element.143), channel_id=1, source_target_pairs={{0,1},{1,0},{2,3},{3,2},{4,5},{5,4},{6,7},{7,6},{8,9},{9,8},{10,11... | collective-permute-start | bytes 1572872 | tf_op jit(solution)/shard_map/ppermute | solution.py:72
  164.5 0.1 collective-permute-start.16
  164.6 1.5 collective-permute-done.16.near_ref
  166.0 0.3 shard_map.154
  166.4 13.1 %all_to_all.110 = f32[32,1,128]{2,1,0:T(1,128)S(1)} all-to-all(f32[32,1,128]{2,1,0:T(1,128)S(1)} %bitcast.80), channel_id=1, replica_groups=mesh['solver'=4,'space'=8] {'solver','space'}, dimensions={0} | all-to-all | bytes 32768 | tf_op jit(solution)/shard_map/all_to_all | solution.py:55
  179.5 2.4 %shard_map.155 = (f32[4096,128]{1,0:T(8,128)S(1)}, f32[256,512]{1,0:T(8,128)S(1)}, f32[256,512]{1,0:T(8,128)S(1)}) custom-call(s32[1]{0:T(128)} %bitcast.refs_0_.me_ref, f32[4096,128]{1,0:T(8,128)S(1)} %get-tuple-element.142.refs_1_, f32[256,512]{1,0:T(8,128)S(1)} %collective-permute-done.15.refs_2_, f32[256,512]{1,0:T(8,128)S(1)} %collective-permute-done.17.refs_3_, ...), custom_call_target="tpu_custom_call" | custom-call | tf_op jit(solution)/shard_map/pallas_call | solution.py:694
  181.9 0.1 collective-permute-start.18
  182.0 0.9 collective-permute-start.19
  182.8 0.3 shard_map.156.refs_7_
  183.2 0.7 collective-permute-done.18.refs_2_
  183.9 7.4 %shard_map.157 = (f32[1024,512]{1,0:T(8,128)}, f32[32,128]{1,0:T(8,128)S(1)}) custom-call(s32[1]{0:T(128)} %bitcast.refs_0_.me_ref, f32[4096,128]{1,0:T(8,128)S(1)} %get-tuple-element.153.refs_1_, f32[256,512]{1,0:T(8,128)S(1)} %collective-permute-done.18.refs_2_, f32[256,512]{1,0:T(8,128)S(1)} %collective-permute-done.19.refs_3_, ...), custom_call_target="tpu_custom_call" | custom-call | tf_op jit(solution)/shard_map/pallas_call | solution.py:694
  191.3 24.9 %all_to_all.111 = f32[32,1,128]{2,1,0:T(1,128)S(1)} all-to-all(f32[32,1,128]{2,1,0:T(1,128)S(1)} %bitcast.78), channel_id=1, replica_groups=mesh['solver'=4,'space'=8] {'solver','space'}, dimensions={0} | all-to-all | bytes 32768 | tf_op jit(solution)/shard_map/all_to_all | solution.py:55
  216.2 2.5 %shard_map.158 = (f32[6,1024]{1,0:T(8,128)S(1)}, f32[6,1024]{1,0:T(8,128)}, f32[32,128]{1,0:T(8,128)}) custom-call(f32[32,128]{1,0:T(8,128)S(1)} %bitcast.65, s32[1,1024]{1,0:T(1,128)S(1)} %bitcast.70, s32[1,1024]{1,0:T(1,128)S(1)} %get-tuple-element.124.rank_ref, f32[3,1024]{1,0:T(4,128)S(1)} %copy-done.6, f32[6,1024]{1,0:T(8,128)S(1)} %get-tuple-element.148.state_ref, ...), custom_call_target="tpu_custom_call" | custom-call | tf_op jit(solution)/shard_map/pallas_call | solution.py:762
  218.7 2.5 %all-to-all-start.8 = ((f32[32,1,128]{2,1,0:T(1,128)}), f32[32,1,128]{2,1,0:T(1,128)S(1)}, u32[]{:S(2)}, u32[]{:S(2)}) async-start(f32[32,1,128]{2,1,0:T(1,128)} %bitcast.35), calls=%async_computation.8 | async-start | bytes 32768 | tf_op jit(solution)/shard_map/all_to_all | solution.py:55
  221.2 1.1 shard_map.160
  222.3 6.1 %all-to-all-done.8 = f32[32,1,128]{2,1,0:T(1,128)S(1)} async-done(((f32[32,1,128]{2,1,0:T(1,128)}), f32[32,1,128]{2,1,0:T(1,128)S(1)}, u32[]{:S(2)}, u32[]{:S(2)}) %all-to-all-start.8) | async-done | bytes 16416 | tf_op jit(solution)/shard_map/all_to_all | solution.py:55
  228.4 4.0 %shard_map.159 = f32[6,1024]{1,0:T(8,128)} custom-call(f32[32,128]{1,0:T(8,128)S(1)} %bitcast.71, f32[32,128]{1,0:T(8,128)S(1)} %bitcast.59, f32[6,1024]{1,0:T(8,128)S(1)} %get-tuple-element.163.output_ref, f32[6,32,1024]{2,1,0:T(8,128)S(1)} %bitcast.55, f32[6,1024]{1,0:T(8,128)S(1)} %get-tuple-element.129.output_ref.last_ref), custom_call_target="tpu_custom_call" | custom-call | tf_op jit(solution)/shard_map/pallas_call | solution.py:784
  (30 shorter events, 0.1 us)
Async XLA Ops:
  0.6 2.6 %copy-start.8 = (s32[1024,1]{0,1:T(1,128)S(1)}, s32[1024,1]{0,1:T(1,128)}, u32[]{:S(2)}) copy-start(s32[1024,1]{0,1:T(1,128)} %param.19) | copy-start | bytes 12292
  0.6 2.6 %copy-start.6 = (f32[3,1024]{1,0:T(4,128)S(1)}, f32[3,1024]{1,0:T(4,128)}, u32[]{:S(2)}) copy-start(f32[3,1024]{1,0:T(4,128)} %normals_ref.7) | copy-start | bytes 36868
  0.7 2.6 %copy-start.4 = (f32[6,1024]{1,0:T(8,128)S(1)}, f32[6,1024]{1,0:T(8,128)}, u32[]{:S(2)}) copy-start(f32[6,1024]{1,0:T(8,128)} %state_ref.4) | copy-start | bytes 73732
  0.7 2.6 %copy-start.9 = (s32[1024]{0:T(1024)S(1)}, s32[1024]{0:T(1024)}, u32[]{:S(2)}) copy-start(s32[1024]{0:T(1024)} %param.20) | copy-start | bytes 12292
  2.0 21.5 %collective-permute-start = (f32[256,512]{1,0:T(8,128)S(1)}, f32[256,512]{1,0:T(8,128)S(1)}, u32[]{:S(2)}, u32[]{:S(2)}) collective-permute-start(f32[256,512]{1,0:T(8,128)S(1)} %get-tuple-element.84), channel_id=1, source_target_pairs={{0,1},{1,0},{2,3},{3,2},{4,5},{5,4},{6,7},{7,6},{8,9},{9,8},{10,11... | collective-permute-start | bytes 1572872 | tf_op jit(solution)/shard_map/ppermute | solution.py:72
  2.6 21.0 %collective-permute-start.1 = (f32[256,512]{1,0:T(8,128)S(1)}, f32[256,512]{1,0:T(8,128)S(1)}, u32[]{:S(2)}, u32[]{:S(2)}) collective-permute-start(f32[256,512]{1,0:T(8,128)S(1)} %get-tuple-element.85), channel_id=1, source_target_pairs={{1,2},{3,4},{5,6},{7,8},{9,10},{11,12},{13,14},{15,16},{17,18},{19... | collective-permute-start | bytes 1572872 | tf_op jit(solution)/shard_map/ppermute | solution.py:71
  23.5 11.0 %copy-start.3 = (f32[3,8,4,256]{3,2,1,0:T(4,128)S(1)}, f32[3,8,4,256]{3,2,1,0:T(4,128)}, u32[]{:S(2)}) copy-start(f32[3,8,4,256]{3,2,1,0:T(4,128)} %start_ref.7) | copy-start | bytes 294916
  23.5 10.9 %copy-start.5 = (f32[3,8,4,256]{3,2,1,0:T(4,128)S(1)}, f32[3,8,4,256]{3,2,1,0:T(4,128)}, u32[]{:S(2)}) copy-start(f32[3,8,4,256]{3,2,1,0:T(4,128)} %load_ref.1) | copy-start | bytes 294916
  23.6 10.9 %copy-start.7 = (f32[8,4,256]{2,1,0:T(4,128)S(1)}, f32[8,4,256]{2,1,0:T(4,128)}, u32[]{:S(2)}) copy-start(f32[8,4,256]{2,1,0:T(4,128)} %stiff_in_ref.1) | copy-start | bytes 98308
  23.6 11.7 %copy-start.1 = (f32[32,6,1024]{2,0,1:T(8,128)S(1)}, f32[32,6,1024]{2,0,1:T(8,128)}, u32[]{:S(2)}) copy-start(f32[32,6,1024]{2,0,1:T(8,128)} %param.22) | copy-start | bytes 2359300
  32.1 20.6 %collective-permute-start.3 = (f32[256,512]{1,0:T(8,128)S(1)}, f32[256,512]{1,0:T(8,128)S(1)}, u32[]{:S(2)}, u32[]{:S(2)}) collective-permute-start(f32[256,512]{1,0:T(8,128)S(1)} %get-tuple-element.91), channel_id=1, source_target_pairs={{1,2},{3,4},{5,6},{7,8},{9,10},{11,12},{13,14},{15,16},{17,18},{19... | collective-permute-start | bytes 1572872 | tf_op jit(solution)/shard_map/ppermute | solution.py:71
  32.8 19.9 %collective-permute-start.2 = (f32[256,512]{1,0:T(8,128)S(1)}, f32[256,512]{1,0:T(8,128)S(1)}, u32[]{:S(2)}, u32[]{:S(2)}) collective-permute-start(f32[256,512]{1,0:T(8,128)S(1)} %get-tuple-element.90), channel_id=1, source_target_pairs={{0,1},{1,0},{2,3},{3,2},{4,5},{5,4},{6,7},{7,6},{8,9},{9,8},{10,11... | collective-permute-start | bytes 1572872 | tf_op jit(solution)/shard_map/ppermute | solution.py:72
  34.6 18.0 %collective-permute-start.4 = (f32[144,256]{1,0:T(8,128)S(1)}, f32[144,256]{1,0:T(8,128)S(1)}, u32[]{:S(2)}, u32[]{:S(2)}) collective-permute-start(f32[144,256]{1,0:T(8,128)S(1)} %get-tuple-element.97), channel_id=1, source_target_pairs={{1,2},{3,4},{5,6},{7,8},{9,10},{11,12},{13,14},{15,16},{17,18},{19... | collective-permute-start | bytes 442376 | tf_op jit(solution)/shard_map/ppermute | solution.py:71
  55.1 17.9 %collective-permute-start.7 = (f32[256,512]{1,0:T(8,128)S(1)}, f32[256,512]{1,0:T(8,128)S(1)}, u32[]{:S(2)}, u32[]{:S(2)}) collective-permute-start(f32[256,512]{1,0:T(8,128)S(1)} %get-tuple-element.105), channel_id=1, source_target_pairs={{1,2},{3,4},{5,6},{7,8},{9,10},{11,12},{13,14},{15,16},{17,18},{19... | collective-permute-start | bytes 1572872 | tf_op jit(solution)/shard_map/ppermute | solution.py:71
  55.8 17.2 %collective-permute-start.5 = (f32[256,512]{1,0:T(8,128)S(1)}, f32[256,512]{1,0:T(8,128)S(1)}, u32[]{:S(2)}, u32[]{:S(2)}) collective-permute-start(f32[256,512]{1,0:T(8,128)S(1)} %get-tuple-element.103), channel_id=1, source_target_pairs={{0,1},{1,0},{2,3},{3,2},{4,5},{5,4},{6,7},{7,6},{8,9},{9,8},{10,11... | collective-permute-start | bytes 1572872 | tf_op jit(solution)/shard_map/ppermute | solution.py:72
  57.7 1.7 collective-permute-start.6
  75.4 5.8 %collective-permute-start.9 = (f32[256,512]{1,0:T(8,128)S(1)}, f32[256,512]{1,0:T(8,128)S(1)}, u32[]{:S(2)}, u32[]{:S(2)}) collective-permute-start(f32[256,512]{1,0:T(8,128)S(1)} %get-tuple-element.114), channel_id=1, source_target_pairs={{1,2},{3,4},{5,6},{7,8},{9,10},{11,12},{13,14},{15,16},{17,18},{19... | collective-permute-start | bytes 1572872 | tf_op jit(solution)/shard_map/ppermute | solution.py:71
  76.1 5.1 %collective-permute-start.8 = (f32[256,512]{1,0:T(8,128)S(1)}, f32[256,512]{1,0:T(8,128)S(1)}, u32[]{:S(2)}, u32[]{:S(2)}) collective-permute-start(f32[256,512]{1,0:T(8,128)S(1)} %get-tuple-element.112), channel_id=1, source_target_pairs={{0,1},{1,0},{2,3},{3,2},{4,5},{5,4},{6,7},{7,6},{8,9},{9,8},{10,11... | collective-permute-start | bytes 1572872 | tf_op jit(solution)/shard_map/ppermute | solution.py:72
  83.6 41.5 %copy-start.2 = (f32[32,6,1024]{2,0,1:T(8,128)S(1)}, f32[32,6,1024]{2,0,1:T(8,128)}, u32[]{:S(2)}) copy-start(f32[32,6,1024]{2,0,1:T(8,128)} %param.23) | copy-start | bytes 2359300
  83.6 51.4 %collective-permute-start.10 = (f32[256,512]{1,0:T(8,128)S(1)}, f32[256,512]{1,0:T(8,128)S(1)}, u32[]{:S(2)}, u32[]{:S(2)}) collective-permute-start(f32[256,512]{1,0:T(8,128)S(1)} %get-tuple-element.121), channel_id=1, source_target_pairs={{0,1},{1,0},{2,3},{3,2},{4,5},{5,4},{6,7},{7,6},{8,9},{9,8},{10,11... | collective-permute-start | bytes 1572872 | tf_op jit(solution)/shard_map/ppermute | solution.py:72
  91.3 43.8 %collective-permute-start.11 = (f32[256,512]{1,0:T(8,128)S(1)}, f32[256,512]{1,0:T(8,128)S(1)}, u32[]{:S(2)}, u32[]{:S(2)}) collective-permute-start(f32[256,512]{1,0:T(8,128)S(1)} %get-tuple-element.122), channel_id=1, source_target_pairs={{1,2},{3,4},{5,6},{7,8},{9,10},{11,12},{13,14},{15,16},{17,18},{19... | collective-permute-start | bytes 1572872 | tf_op jit(solution)/shard_map/ppermute | solution.py:71
  92.0 43.1 %copy-start = (f32[4,256,512]{2,1,0:T(8,128)S(1)}, f32[4,256,512]{2,1,0:T(8,128)}, u32[]{:S(2)}) copy-start(f32[4,256,512]{2,1,0:T(8,128)} %param.14) | copy-start | bytes 6291460
  143.8 2.7 %collective-permute-start.13 = (f32[256,512]{1,0:T(8,128)S(1)}, f32[256,512]{1,0:T(8,128)S(1)}, u32[]{:S(2)}, u32[]{:S(2)}) collective-permute-start(f32[256,512]{1,0:T(8,128)S(1)} %get-tuple-element.136), channel_id=1, source_target_pairs={{1,2},{3,4},{5,6},{7,8},{9,10},{11,12},{13,14},{15,16},{17,18},{19... | collective-permute-start | bytes 1572872 | tf_op jit(solution)/shard_map/ppermute | solution.py:71
  144.5 2.9 %collective-permute-start.12 = (f32[256,512]{1,0:T(8,128)S(1)}, f32[256,512]{1,0:T(8,128)S(1)}, u32[]{:S(2)}, u32[]{:S(2)}) collective-permute-start(f32[256,512]{1,0:T(8,128)S(1)} %get-tuple-element.135), channel_id=1, source_target_pairs={{0,1},{1,0},{2,3},{3,2},{4,5},{5,4},{6,7},{7,6},{8,9},{9,8},{10,11... | collective-permute-start | bytes 1572872 | tf_op jit(solution)/shard_map/ppermute | solution.py:72
  145.9 0.7 collective-permute-start.14
  149.8 29.6 %collective-permute-start.17 = (f32[256,512]{1,0:T(8,128)S(1)}, f32[256,512]{1,0:T(8,128)S(1)}, u32[]{:S(2)}, u32[]{:S(2)}) collective-permute-start(f32[256,512]{1,0:T(8,128)S(1)} %get-tuple-element.145), channel_id=1, source_target_pairs={{1,2},{3,4},{5,6},{7,8},{9,10},{11,12},{13,14},{15,16},{17,18},{19... | collective-permute-start | bytes 1572872 | tf_op jit(solution)/shard_map/ppermute | solution.py:71
  150.5 28.9 %collective-permute-start.15 = (f32[256,512]{1,0:T(8,128)S(1)}, f32[256,512]{1,0:T(8,128)S(1)}, u32[]{:S(2)}, u32[]{:S(2)}) collective-permute-start(f32[256,512]{1,0:T(8,128)S(1)} %get-tuple-element.143), channel_id=1, source_target_pairs={{0,1},{1,0},{2,3},{3,2},{4,5},{5,4},{6,7},{7,6},{8,9},{9,8},{10,11... | collective-permute-start | bytes 1572872 | tf_op jit(solution)/shard_map/ppermute | solution.py:72
  164.5 1.5 collective-permute-start.16
  181.9 2.0 collective-permute-start.18
  182.0 1.9 collective-permute-start.19
  218.7 9.6 %all-to-all-start.8 = ((f32[32,1,128]{2,1,0:T(1,128)}), f32[32,1,128]{2,1,0:T(1,128)S(1)}, u32[]{:S(2)}, u32[]{:S(2)}) async-start(f32[32,1,128]{2,1,0:T(1,128)} %bitcast.35), calls=%async_computation.8 | async-start | bytes 32768 | tf_op jit(solution)/shard_map/all_to_all | solution.py:55
